TPU v7x, 32 devices: a whole 2x2x4 slice. The times are simulated.
32 devices in a mesh: pipe: 2 (over core), dp: 4 (over z), mp: 4 (over y, x).
Axes of the slice: x: 2, y: 2, z: 4, core: 2. Of those that a mesh axis runs over, the one named last changes fastest.
Arguments:
- hidden_states: bfloat16 [16, 64, 4096], P('dp'), may hold values from -6 to 6
- up_weight: bfloat16 [2, 4096, 7168], P('pipe', 'dp', 'mp'), may hold values from -0.09375 to 0.09375
- down_weight: bfloat16 [2, 7168, 4096], P('pipe', 'mp', 'dp'), may hold values from -0.0625 to 0.0625
- layer_gain: float32 [2, 4096], P('pipe'), may hold values from 0.5 to 1.5
- final_gain: float32 [4096], replicated, may hold values from 0.5 to 1.5
- unembedding: bfloat16 [32768, 4096], P(('pipe', 'mp')), may hold values from -32 to 32
- target_ids: int32 [16, 64], P('dp'), may hold values from 0 to 32767
- response_masks: int32 [16, 64], P('dp'), may hold values from 0 to 1, as said below
- anchor_logps: float32 [16, 64], P('dp'), may hold values from -14 to -10
- pairing: int32 [4, 4], P('dp'), may hold values from 0 to 3, each once within a row
Outputs:
- token_logps: float32 [16, 64], P('dp')
- seq_logps: float32 [16], P('dp')
- pair_losses: float32 [8], P('dp')
Inputs may be any that keep to these rules, and one draw needn't show every extreme that they name: response_masks is 1 on one unbroken run of at least one position per sequence, starting at or after position 8, and 0 elsewhere.
All inputs are finite; a program needn't handle non-finite values.
Results may differ from a plain program's by a relative error of at most 0.0075.
Values may be sent and summed in bfloat16 or wider, within the bound.
A program may use at most 192 MiB of HBM per device.

v0:
```python
import functools
import jax
import jax.numpy as jnp
from jax import lax
from jax.experimental import pallas as pl
from jax.experimental.pallas import tpu as pltpu
from jax.sharding import PartitionSpec as P

SEQ_MB = 1

epsilon = 1e-05
ipo_tau = 0.5
VP = ("pipe", "mp")
MESH = pl.DeviceIdType.MESH
PIECES = 8


def remote(src, dst, send_sem, recv_sem, target):
    return pltpu.make_async_remote_copy(
        src_ref=src,
        dst_ref=dst,
        send_sem=send_sem,
        recv_sem=recv_sem,
        device_id=target,
        device_id_type=MESH,
    )


def greet(axes):
    barrier = pltpu.get_barrier_semaphore()
    total = 0
    for axis in axes:
        size = lax.axis_size(axis)
        here = lax.axis_index(axis)
        for k in range(1, size):
            pl.semaphore_signal(
                barrier, inc=1, device_id={axis: lax.rem(here + k, size)}, device_id_type=MESH
            )
        total += size - 1
    pl.semaphore_wait(barrier, total)


def chunk_rows(index, size):
    return pl.ds(pl.multiple_of(index * size, 8), size)


def spread(full, size, mp_sems, pipe_sems):
    (mp_send, mp_recv), (pipe_send, pipe_recv) = mp_sems, pipe_sems
    count = lax.axis_size("mp")
    m, p = lax.axis_index("mp"), lax.axis_index("pipe")

    def to_mp(k, owner):
        rows = full.at[chunk_rows(p * count + owner, size)]
        return remote(rows, rows, mp_send.at[k], mp_recv.at[k], {"mp": lax.rem(m + k, count)})

    def to_pipe(k, pipe):
        rows = full.at[chunk_rows(pipe * count + lax.rem(m - k + count, count), size)]
        return remote(rows, rows, pipe_send.at[k], pipe_recv.at[k], {"pipe": 1 - p})

    for k in range(1, count):
        to_mp(k, m).start()
    to_pipe(0, p).start()
    for k in range(1, count):
        to_mp(k, lax.rem(m - k + count, count)).wait_recv()
        to_pipe(k, p).start()
    for k in range(count):
        to_pipe(k, 1 - p).wait_recv()
    for k in range(1, count):
        to_mp(k, m).wait_send()
    for k in range(count):
        to_pipe(k, p).wait_send()


def gather_sum(part, size, near, far, sent, sems):
    near_send, near_recv, far_send, far_recv = sems
    count = lax.axis_size("mp")
    m, p = lax.axis_index("mp"), lax.axis_index("pipe")
    order = list(range(1, count)) + [0]

    def to_core(k):
        rows = part.at[chunk_rows((1 - p) * count + lax.rem(m + k, count), size)]
        return remote(rows, near.at[k], near_send.at[k], near_recv.at[k], {"pipe": 1 - p})

    def to_chip(k):
        return remote(
            sent.at[k], far.at[k], far_send.at[k], far_recv.at[k], {"mp": lax.rem(m + k, count)}
        )

    for k in order:
        to_core(k).start()
    for k in order:
        to_core(k).wait_recv()
        own = part[chunk_rows(p * count + lax.rem(m + k, count), size), :].astype(jnp.float32)
        own = own + near[k].astype(jnp.float32)
        if k > 0:
            sent[k] = own.astype(sent.dtype)
            to_chip(k).start()
    for k in range(1, count):
        to_chip(k).wait_recv()
        own = own + far[k].astype(jnp.float32)
    for k in range(1, count):
        to_chip(k).wait_send()
    for k in order:
        to_core(k).wait_send()
    return own


def share_sum(slots, send, recv):
    count = lax.axis_size("dp")
    d = lax.axis_index("dp")

    def hop(k):
        return remote(
            slots.at[0], slots.at[k], send.at[k], recv.at[k], {"dp": lax.rem(d + k, count)}
        )

    for k in range(1, count):
        hop(k).start()
    total = slots[0]
    for k in range(1, count):
        hop(k).wait_recv()
        total = total + slots[k]
    for k in range(1, count):
        hop(k).wait_send()
    return total


def first_kernel(
    x_ref, gain_ref, blocks_ref, full_ref, normed_ref, n_send, n_recv, x_send, x_recv, ms, mr, ps, pr
):
    count = lax.axis_size("dp")
    d = lax.axis_index("dp")
    v = lax.axis_index(("pipe", "mp"))
    part, width = x_ref.shape
    block = width // count
    greet(("dp", "mp", "pipe"))
    wide = x_ref[...].astype(jnp.float32)
    scale = lax.rsqrt(jnp.mean(wide * wide, axis=-1, keepdims=True) + epsilon)
    normed_ref[...] = (wide * scale * gain_ref[...]).astype(normed_ref.dtype)

    def columns(owner):
        return pl.ds(pl.multiple_of(owner * block, 128), block)

    def normed_hop(k, owner):
        to = lax.rem(d + k, count)
        return remote(
            normed_ref.at[:, columns(to)],
            full_ref.at[chunk_rows(v * count + owner, part)],
            n_send.at[k],
            n_recv.at[k],
            {"dp": to},
        )

    def plain_hop(k, owner):
        to = lax.rem(d + k, count)
        return remote(
            x_ref.at[:, columns(to)],
            blocks_ref.at[chunk_rows(owner, part)],
            x_send.at[k],
            x_recv.at[k],
            {"dp": to},
        )

    for k in range(1, count):
        normed_hop(k, d).start()
    for k in range(1, count):
        plain_hop(k, d).start()
    full_ref[chunk_rows(v * count + d, part), :] = normed_ref[:, columns(d)]
    blocks_ref[chunk_rows(d, part), :] = x_ref[:, columns(d)]
    for k in range(1, count):
        normed_hop(k, lax.rem(d - k + count, count)).wait_recv()
    spread(full_ref, part * count, (ms, mr), (ps, pr))
    for k in range(1, count):
        plain_hop(k, lax.rem(d - k + count, count)).wait_recv()
    for k in range(1, count):
        normed_hop(k, d).wait_send()
        plain_hop(k, d).wait_send()


def middle_kernel(
    width, part_ref, resid_ref, gain_ref, blocks_ref, full_ref,
    near, far, sent, slots, ns, nr, fs, fr, qs, qr, ms, mr, ps, pr,
):
    v = lax.axis_index(("pipe", "mp"))
    size = resid_ref.shape[0]
    greet(("dp", "mp", "pipe"))
    summed = gather_sum(part_ref, size, near, far, sent, (ns, nr, fs, fr))
    value = (resid_ref[...].astype(jnp.float32) + summed).astype(jnp.bfloat16)
    blocks_ref[...] = value
    wide = value.astype(jnp.float32)
    slots[0] = lax.dot_general(
        jnp.ones((8, wide.shape[1]), jnp.float32),
        wide * wide,
        (((1,), (1,)), ((), ())),
        precision=lax.Precision.HIGHEST,
        preferred_element_type=jnp.float32,
    )
    scale = lax.rsqrt(share_sum(slots, qs, qr) / width + epsilon)
    scale = jnp.transpose(scale)[:, :1]
    wide = blocks_ref[...].astype(jnp.float32)
    full_ref[chunk_rows(v, size), :] = (wide * scale * gain_ref[...]).astype(full_ref.dtype)
    spread(full_ref, size, (ms, mr), (ps, pr))


def last_kernel(
    part_ref, resid_ref, gain_ref, full_ref,
    near, far, sent, blocks, fin, ns, nr, fs, fr, hs, hr, ms, mr, ps, pr,
):
    count = lax.axis_size("dp")
    d = lax.axis_index("dp")
    v = lax.axis_index(("pipe", "mp"))
    size, block = resid_ref.shape
    part = size // count
    greet(("dp", "mp", "pipe"))
    summed = gather_sum(part_ref, size, near, far, sent, (ns, nr, fs, fr))
    blocks[...] = (resid_ref[...].astype(jnp.float32) + summed).astype(jnp.bfloat16)

    def hop(k, owner):
        to = lax.rem(d + k, count)
        return remote(
            blocks.at[chunk_rows(to, part)], fin.at[owner], hs.at[k], hr.at[k], {"dp": to}
        )

    for k in range(1, count):
        hop(k, d).start()
    fin[d] = blocks[chunk_rows(d, part), :]
    for k in range(1, count):
        hop(k, lax.rem(d - k + count, count)).wait_recv()
    total = 0.0
    for g in range(count):
        wide = fin[g].astype(jnp.float32)
        total = total + jnp.sum(wide * wide, axis=1, keepdims=True)
    scale = lax.rsqrt(total / (block * count) + epsilon)
    for g in range(count):
        cut = slice(g * block, (g + 1) * block)
        full_ref[chunk_rows(v, part), cut] = (
            fin[g].astype(jnp.float32) * scale * gain_ref[:, cut]
        ).astype(full_ref.dtype)
    spread(full_ref, part, (ms, mr), (ps, pr))
    for k in range(1, count):
        hop(k, d).wait_send()


def stats_kernel(stats_ref, counts_ref, full_ref, total_ref, slots, qs, qr, ms, mr, ps, pr):
    v = lax.axis_index(("pipe", "mp"))
    size = stats_ref.shape[0]
    greet(("dp", "mp", "pipe"))
    slots[0] = counts_ref[...]
    full_ref[chunk_rows(v, size), :] = stats_ref[...]
    total_ref[...] = share_sum(slots, qs, qr)
    spread(full_ref, size, (ms, mr), (ps, pr))


def chain_kernel(h_ref, out_ref, arrived, summed, rs, rr, gs, gr):
    count = lax.axis_size("dp")
    d = lax.axis_index("dp")
    half = h_ref.shape[0] // 2
    rows = half // PIECES
    right, left = lax.rem(d + 1, count), lax.rem(d + count - 1, count)
    barrier = pltpu.get_barrier_semaphore()
    for has, who in ((d > 0, left), (d < count - 1, right)):

        @pl.when(has)
        def _():
            pl.semaphore_signal(barrier, inc=1, device_id={"dp": who}, device_id_type=MESH)

    ends = (d > 0).astype(jnp.int32) + (d < count - 1).astype(jnp.int32)
    pl.semaphore_wait(barrier, ends)

    hops = (d, count - 1 - d)

    def cut(way, c):
        return pl.ds(pl.multiple_of((1 - way) * half + c * rows, 16), rows)

    def onward_copy(way, c, source):
        to = (right, left)[way]
        return remote(source, arrived.at[way, c], rs.at[way, c], rr.at[way, c], {"dp": to})

    def back_copy(way, c):
        spot = out_ref.at[cut(way, c)]
        to = (left, right)[way]
        return remote(spot, spot, gs.at[way, c], gr.at[way, c], {"dp": to})

    for way in range(2):

        @pl.when(hops[way] == 0)
        def _():
            for c in range(PIECES):
                onward_copy(way, c, h_ref.at[cut(way, c)]).start()

    def step(t, carry):
        for way in range(2):
            before = hops[way]
            c = t - before

            @pl.when((before > 0) & (c >= 0) & (c < PIECES))
            def _():
                onward_copy(way, c, summed.at[way, c]).wait_recv()
                total = arrived[way, c] + h_ref[cut(way, c), :]

                @pl.when(before < count - 1)
                def _():
                    summed[way, c] = total
                    onward_copy(way, c, summed.at[way, c]).start()

                @pl.when(before == count - 1)
                def _():
                    out_ref[cut(way, c), :] = (total / (1.0 + jnp.exp(-total))).astype(
                        out_ref.dtype
                    )
                    back_copy(way, c).start()

        for way in range(2):
            after = count - 1 - hops[way]
            g = t - (count - 1) - after

            @pl.when((after > 0) & (g >= 0) & (g < PIECES))
            def _():
                back_copy(way, g).wait_recv()

                @pl.when(after < count - 1)
                def _():
                    back_copy(way, g).start()

        return carry

    lax.fori_loop(0, PIECES + 2 * (count - 1), step, 0)
    for way in range(2):

        @pl.when(hops[way] < count - 1)
        def _():
            for c in range(PIECES):
                onward_copy(way, c, summed.at[way, c]).wait_send()

        @pl.when(hops[way] > 0)
        def _():
            for c in range(PIECES):
                back_copy(way, c).wait_send()


def call(kernel, name, ident, outs, scratch, *args):
    spec = pl.BlockSpec(memory_space=pltpu.VMEM)
    return pl.pallas_call(
        kernel,
        name=name,
        out_shape=outs,
        in_specs=[spec] * len(args),
        out_specs=jax.tree.map(lambda _: spec, outs),
        scratch_shapes=scratch,
        compiler_params=pltpu.CompilerParams(collective_id=ident, has_side_effects=True),
    )(*args)


def sems(*shape):
    return [pltpu.SemaphoreType.DMA(shape)] * 2


def shards(
    hidden_states,
    up_weight,
    down_weight,
    layer_gain,
    final_gain,
    unembedding,
    target_ids,
    response_masks,
    anchor_logps,
    pairing,
):
    seq_count, length, model_width = hidden_states.shape
    groups = lax.axis_size("dp")
    vp_size = lax.axis_size("pipe") * lax.axis_size("mp")
    vp_index = lax.axis_index(VP)
    dp_index = lax.axis_index("dp")
    pipe_index = lax.axis_index("pipe")
    rows = seq_count * length
    part = rows // vp_size
    block = model_width // groups
    mask_values = response_masks.astype(jnp.float32)
    local_counts = jnp.sum(mask_values, axis=1)
    count = lax.axis_size("mp")
    bf16 = jnp.bfloat16
    spread_sems = sems(count) + sems(count)
    reach_sems = sems(count) + sems(count)
    buffers = [pltpu.VMEM((count, part, block), jnp.float32) for part in [rows // vp_size * groups]] * 3

    up_own, down_own = up_weight[0], down_weight[0]
    half = up_own.shape[1] // 2
    away = (1 - pipe_index) * half
    keep = pipe_index * half
    swap = [(0, 1), (1, 0)]
    gain_other = lax.ppermute(layer_gain, "pipe", swap)
    up_other = lax.ppermute(lax.dynamic_slice_in_dim(up_own, away, half, 1), "pipe", swap)
    down_other = lax.ppermute(lax.dynamic_slice_in_dim(down_own, away, half, 0), "pipe", swap)
    up_mine = lax.dynamic_slice_in_dim(up_own, keep, half, 1)
    down_mine = lax.dynamic_slice_in_dim(down_own, keep, half, 0)

    def section_of(s):
        own = pipe_index == s
        gain = jnp.where(own, layer_gain[0], gain_other[0])
        return (
            lax.dynamic_slice_in_dim(gain, dp_index * block, block, 0),
            jnp.where(own, up_mine, up_other),
            jnp.where(own, down_mine, down_other),
        )

    mine = lax.dynamic_slice_in_dim(
        hidden_states.reshape(rows, model_width), vp_index * part, part, 0
    )
    size = part * groups
    total_rows = rows * groups
    blocks, full = call(
        first_kernel,
        "first",
        0,
        [
            jax.ShapeDtypeStruct((size, block), bf16),
            jax.ShapeDtypeStruct((total_rows, block), bf16),
        ],
        [pltpu.VMEM((part, model_width), bf16)] + sems(groups) + sems(groups) + spread_sems,
        mine,
        jnp.where(pipe_index == 0, layer_gain, gain_other),
    )
    for s in range(2):
        gain, up, down = section_of(s)
        hidden = jnp.dot(full, up, preferred_element_type=jnp.float32)
        piece = hidden.shape[0] // (2 * PIECES)
        active = call(
            chain_kernel,
            "chain",
            1,
            jax.ShapeDtypeStruct(hidden.shape, bf16),
            [pltpu.VMEM((2, PIECES, piece, half), jnp.float32)] * 2 + sems(2, PIECES) + sems(2, PIECES),
            hidden,
        )
        out = jnp.dot(active, down, preferred_element_type=jnp.float32)
        if s == 0:
            gain = section_of(1)[0]
            blocks, full = call(
                functools.partial(middle_kernel, model_width),
                "middle",
                2,
                [
                    jax.ShapeDtypeStruct((size, block), bf16),
                    jax.ShapeDtypeStruct((total_rows, block), bf16),
                ],
                buffers
                + [pltpu.VMEM((groups, 8, size), jnp.float32)]
                + reach_sems
                + sems(groups)
                + spread_sems,
                out,
                blocks,
                gain[None],
            )
        else:
            normed_final = call(
                last_kernel,
                "last",
                3,
                jax.ShapeDtypeStruct((rows, model_width), bf16),
                buffers
                + [pltpu.VMEM((size, block), bf16), pltpu.VMEM((groups, part, block), bf16)]
                + reach_sems
                + sems(groups)
                + spread_sems,
                out,
                blocks,
                final_gain[None],
            )
    logits = lax.dot_general(
        normed_final, unembedding, (((1,), (1,)), ((), ())), preferred_element_type=jnp.float32
    )
    vocab_start = vp_index * unembedding.shape[0]
    local_ids = target_ids.reshape(-1) - vocab_start
    columns = lax.broadcasted_iota(jnp.int32, logits.shape, 1)
    picked = jnp.sum(jnp.where(columns == local_ids[:, None], logits, 0.0), axis=1)
    local_top = jnp.max(logits, axis=1)
    local_sum = jnp.sum(jnp.exp(logits - local_top[:, None]), axis=1)
    stats = jnp.pad(jnp.stack([local_top, local_sum, picked]), ((0, 5), (0, 0)))
    padded = jnp.pad(local_counts[None], ((0, 7), (0, -seq_count % 128)))
    stats, counts = call(
        stats_kernel,
        "stats",
        4,
        [
            jax.ShapeDtypeStruct((vp_size * 8, rows), jnp.float32),
            jax.ShapeDtypeStruct(padded.shape, jnp.float32),
        ],
        [pltpu.VMEM((groups,) + padded.shape, jnp.float32)] + sems(groups) + spread_sems,
        stats,
        padded,
    )
    stats = stats.reshape(vp_size, 8, rows)
    counts = counts[0, :seq_count]
    top_value = jnp.max(stats[:, 0], axis=0)
    exp_total = jnp.sum(stats[:, 1] * jnp.exp(stats[:, 0] - top_value), axis=0)
    picked_all = jnp.sum(stats[:, 2], axis=0)
    token_logps = (picked_all - top_value - jnp.log(exp_total)).reshape(seq_count, length)

    divisor = jnp.repeat(counts / (groups * SEQ_MB), SEQ_MB)
    policy = jnp.sum(mask_values * token_logps, axis=1) / divisor
    anchor = jnp.sum(mask_values * anchor_logps, axis=1) / divisor
    log_gaps = policy - anchor
    positions = jnp.arange(seq_count, dtype=jnp.int32)
    chosen = jnp.sum(
        jnp.where(pairing[0, 0::2][:, None] == positions[None, :], log_gaps[None, :], 0.0), axis=1
    )
    rejected = jnp.sum(
        jnp.where(pairing[0, 1::2][:, None] == positions[None, :], log_gaps[None, :], 0.0), axis=1
    )
    losses = (chosen - rejected - 0.5 / ipo_tau) ** 2
    return (token_logps, policy, losses)


def solution(mesh):
    return jax.shard_map(
        shards,
        mesh=mesh,
        in_specs=(
            P("dp", None, None),
            P("pipe", "dp", "mp"),
            P("pipe", "mp", "dp"),
            P("pipe", None),
            P(),
            P(("pipe", "mp"), None),
            P("dp", None),
            P("dp", None),
            P("dp", None),
            P("dp", None),
        ),
        out_specs=(P("dp", None), P("dp"), P("dp")),
        check_vma=False,
    )
```

profile of v0, /device:TPU:0, one launch (start us, length us, event | category | flops | bytes accessed | tf_op | source)
XLA Modules:
  0.0 406.7 jit_solution(17871407408044581722)
XLA Ops:
  0.6 0.0 copy-start
  0.6 0.6 collective-permute-start
  1.2 0.0 copy-start.2
  1.2 3.0 dynamic-slice_bitcast_fusion.1
  4.3 0.0 copy-start.7
  4.3 0.1 collective-permute-start.1
  4.4 0.0 copy-done.2
  4.4 1.4 dynamic-slice_bitcast_fusion
  5.8 0.5 collective-permute-start.2
  6.2 0.0 copy-done
  6.2 0.7 constant_dynamic-slice_fusion.x_ref
  7.0 0.0 copy-done.7
  7.0 0.0 copy-done.4
  7.0 0.1 convert_reduce_fusion
  7.1 0.0 copy-done.8
  7.1 0.1 slice.23
  7.2 0.1 slice.24
  7.3 0.1 sub.59
  7.4 0.6 pad.9.counts_ref
  7.9 0.0 collective-permute-done
  8.0 0.0 copy-done.3
  8.0 0.6 broadcast_select_fusion.gain_ref
  8.6 28.2 %first.1 = (bf16[128,1024]{1,0:T(8,128)(2,1)}, bf16[1024,1024]{1,0:T(8,128)(2,1)}) custom-call(bf16[32,4096]{1,0:T(8,128)(2,1)} %constant_dynamic-slice_fusion.x_ref, f32[1,4096]{1,0:T(1,128)} %broadcast_select_fusion.gain_ref), custom_call_target="tpu_custom_call" | custom-call | tf_op jit(solution)/shard_map/first/pallas_call | solution.py:343
  36.7 0.6 broadcast_select_fusion.1.gain_ref
  37.3 0.0 collective-permute-done.1
  37.4 6.3 %fusion.2.h_ref = f32[1024,896]{1,0:T(8,128)} fusion(bf16[1024,1024]{1,0:T(8,128)(2,1)} %get-tuple-element.9, bf16[1024,896]{1,0:T(8,128)(2,1)} %collective-permute-done.1, pred[]{:T(512)S(6)} %eq.46, bf16[1,1024,1792]{2,1,0:T(8,128)(2,1)} %param.11, s32[]{:T(128)S(6)} %select_n.74), kind=kOutput, calls=%fused_computation.9 | convolution fusion | flops 1879965696 | bytes 9437189 | tf_op jit(solution)/shard_map/dot_general | solution.py:426
  43.6 102.4 %chain.2 = bf16[1024,896]{1,0:T(8,128)(2,1)} custom-call(f32[1024,896]{1,0:T(8,128)} %fusion.2.h_ref), custom_call_target="tpu_custom_call" | custom-call | tf_op jit(solution)/shard_map/chain/pallas_call | solution.py:343
  146.1 0.0 collective-permute-done.2
  146.1 6.4 %fusion.part_ref = f32[1024,1024]{1,0:T(8,128)} fusion(bf16[1024,896]{1,0:T(8,128)(2,1)} %chain.2, bf16[896,1024]{1,0:T(8,128)(2,1)} %collective-permute-done.2, pred[]{:T(512)S(6)} %eq.46, bf16[1,1792,1024]{2,1,0:T(8,128)(2,1)} %param.12, s32[]{:T(128)S(6)} %select_n.74), kind=kOutput, calls=%fused_computation.5 | convolution fusion | flops 1879965696 | bytes 9699333 | tf_op jit(solution)/shard_map/dot_general | solution.py:436
  152.4 51.1 %middle.1 = (bf16[128,1024]{1,0:T(8,128)(2,1)}, bf16[1024,1024]{1,0:T(8,128)(2,1)}) custom-call(f32[1024,1024]{1,0:T(8,128)} %fusion.part_ref, bf16[128,1024]{1,0:T(8,128)(2,1)} %get-tuple-element.10.resid_ref, f32[1,1024]{1,0:T(1,128)} %broadcast_select_fusion.1.gain_ref), custom_call_target="tpu_custom_call" | custom-call | tf_op jit(solution)/shard_map/middle/pallas_call | solution.py:343
  203.5 6.9 %fusion.3.h_ref = f32[1024,896]{1,0:T(8,128)} fusion(bf16[1024,1024]{1,0:T(8,128)(2,1)} %get-tuple-element.11, bf16[1024,896]{1,0:T(8,128)(2,1)} %collective-permute-done.1, pred[]{:T(512)S(6)} %eq.47, bf16[1,1024,1792]{2,1,0:T(8,128)(2,1)} %param.11, s32[]{:T(128)S(6)} %select_n.74), kind=kOutput, calls=%fused_computation.10 | convolution fusion | flops 1879965696 | bytes 9437189 | tf_op jit(solution)/shard_map/dot_general | solution.py:426
  210.4 98.7 %chain.3 = bf16[1024,896]{1,0:T(8,128)(2,1)} custom-call(f32[1024,896]{1,0:T(8,128)} %fusion.3.h_ref), custom_call_target="tpu_custom_call" | custom-call | tf_op jit(solution)/shard_map/chain/pallas_call | solution.py:343
  309.1 6.9 %fusion.1.part_ref = f32[1024,1024]{1,0:T(8,128)} fusion(bf16[1024,896]{1,0:T(8,128)(2,1)} %chain.3, bf16[896,1024]{1,0:T(8,128)(2,1)} %collective-permute-done.2, pred[]{:T(512)S(6)} %eq.47, bf16[1,1792,1024]{2,1,0:T(8,128)(2,1)} %param.12, s32[]{:T(128)S(6)} %select_n.74), kind=kOutput, calls=%fused_computation.6 | convolution fusion | flops 1879965696 | bytes 9699333 | tf_op jit(solution)/shard_map/dot_general | solution.py:436
  316.0 53.0 %last.1 = bf16[256,4096]{1,0:T(8,128)(2,1)} custom-call(f32[1024,1024]{1,0:T(8,128)} %fusion.1.part_ref, bf16[128,1024]{1,0:T(8,128)(2,1)} %get-tuple-element.12.resid_ref, f32[1,4096]{1,0:T(1,128)} %bitcast.58), custom_call_target="tpu_custom_call" | custom-call | tf_op jit(solution)/shard_map/last/pallas_call | solution.py:343
  369.0 17.5 %fusion.24 = (f32[256]{0:T(256)S(1)}, f32[256,4096]{1,0:T(8,128)}) fusion(bf16[256,4096]{1,0:T(8,128)(2,1)} %last.1, bf16[4096,4096]{1,0:T(8,128)(2,1)} %param.15), kind=kOutput, calls=%fused_computation.54 | convolution fusion | flops 8590983168 | bytes 39846912 | tf_op jit(solution)/shard_map/dot_general | solution.py:471
  386.5 3.5 exponential_reduce_fusion
  390.0 0.6 select_maximum_fusion.stats_ref
  390.6 12.2 %stats.1 = (f32[64,256]{1,0:T(8,128)}, f32[8,128]{1,0:T(8,128)}) custom-call(f32[8,256]{1,0:T(8,128)} %select_maximum_fusion.stats_ref, f32[8,128]{1,0:T(8,128)} %pad.9.counts_ref), custom_call_target="tpu_custom_call" | custom-call | tf_op jit(solution)/shard_map/stats/pallas_call | solution.py:343
  402.7 1.0 slice_reduce_fusion
  403.8 0.1 sub.64
  403.9 0.0 copy-done.6
  403.9 0.1 multiply_reduce_fusion
  404.0 1.2 bitcast_divide_fusion.2
  405.2 0.7 fusion.23
  405.9 0.2 fusion.21
  406.1 0.5 add_multiply_fusion
  406.6 0.0 copy-done.5
  406.7 0.0 copy-done.1
  (9 shorter events, 0.0 us)
Async XLA Ops:
  0.6 5.6 %copy-start = (bf16[4,64,4096]{2,1,0:T(8,128)(2,1)S(1)}, bf16[4,64,4096]{2,1,0:T(8,128)(2,1)}, u32[]{:S(2)}) copy-start(bf16[4,64,4096]{2,1,0:T(8,128)(2,1)} %param.10) | copy-start | bytes 6291460
  0.6 7.3 %collective-permute-start = (f32[1,4096]{1,0:T(1,128)}, f32[1,4096]{1,0:T(1,128)S(1)}, u32[]{:S(2)}, u32[]{:S(2)}) collective-permute-start(f32[1,4096]{1,0:T(1,128)} %param.13), channel_id=1, source_target_pairs={{0,16},{16,0},{1,17},{17,1},{2,18},{18,2},{3,19},{19,3},{4,20},{20... | collective-permute-start | bytes 49160 | tf_op jit(solution)/shard_map/ppermute | solution.py:392
  1.2 3.2 copy-start.2
  4.3 2.7 copy-start.7
  4.3 2.7 copy-start.4
  4.3 2.8 copy-start.8
  4.3 3.7 copy-start.3
  4.3 33.1 %collective-permute-start.1 = (bf16[1024,896]{1,0:T(8,128)(2,1)}, bf16[1024,896]{1,0:T(8,128)(2,1)}, u32[]{:S(2)}, u32[]{:S(2)}) collective-permute-start(bf16[1024,896]{1,0:T(8,128)(2,1)} %dynamic-slice_bitcast_fusion.1), channel_id=1, source_target_pairs={{0,16},{16,0},{1,17},{17,1},{2,18},{18,2},{3,19},{19,3},{4,20},{20... | collective-permute-start | bytes 5505032 | tf_op jit(solution)/shard_map/ppermute | solution.py:393
  5.8 140.3 %collective-permute-start.2 = (bf16[896,1024]{1,0:T(8,128)(2,1)}, bf16[896,1024]{1,0:T(8,128)(2,1)}, u32[]{:S(2)}, u32[]{:S(2)}) collective-permute-start(bf16[896,1024]{1,0:T(8,128)(2,1)} %dynamic-slice_bitcast_fusion), channel_id=1, source_target_pairs={{0,16},{16,0},{1,17},{17,1},{2,18},{18,2},{3,19},{19,3},{4,20},{20... | collective-permute-start | bytes 5505032 | tf_op jit(solution)/shard_map/ppermute | solution.py:394
  386.5 20.2 %copy-start.1 = (bf16[4,64,4096]{2,1,0:T(8,128)(2,1)S(1)}, bf16[4,64,4096]{2,1,0:T(8,128)(2,1)}, u32[]{:S(2)}) copy-start(bf16[4,64,4096]{2,1,0:T(8,128)(2,1)} %param.10) | copy-start | bytes 6291460
  386.5 17.4 %copy-start.6 = (f32[4,64]{1,0:T(4,128)S(1)}, f32[4,64]{1,0:T(4,128)}, u32[]{:S(2)}) copy-start(f32[4,64]{1,0:T(4,128)} %param.18) | copy-start | bytes 3076
  403.9 2.8 copy-start.5
where the time goes:
time: 407 us
  Pallas kernels  345 us (85%)
  matrix products  43.9 us (11%)
  other arithmetic  9.22 us (2%)
  local copies, waits for them, and re-layouts  6.13 us (2%)
    pallas_call x6, Pallas kernels, call(): pl.pallas_call(kernel, name=name, out_shape=outs, in_specs=[spec] * len(a...  345 us
    dot_general x1, matrix products, shards(): lax.dot_general(normed_final, unembedding, (((1,), (1,)), ((), ())), pref...  17.5 us
    dot_general x2, matrix products, shards(): out = jnp.dot(active, down, preferred_element_type=jnp.float32)  13.3 us
    dot_general x2, matrix products, shards(): hidden = jnp.dot(full, up, preferred_element_type=jnp.float32)  13.2 us
  transfers between devices with their start and end apart: 3, of which 0 were waited for; matrix products, arithmetic and copies ran while one was open for 3% of the time, Pallas kernels for 32%

commit v1 on v0

--- a/solution.py
+++ b/solution.py
@@ -296,11 +296,11 @@
             @pl.when((before > 0) & (c >= 0) & (c < PIECES))
             def _():
                 onward_copy(way, c, summed.at[way, c]).wait_recv()
-                total = arrived[way, c] + h_ref[cut(way, c), :]
+                total = arrived[way, c].astype(jnp.float32) + h_ref[cut(way, c), :].astype(jnp.float32)
 
                 @pl.when(before < count - 1)
                 def _():
-                    summed[way, c] = total
+                    summed[way, c] = total.astype(summed.dtype)
                     onward_copy(way, c, summed.at[way, c]).start()
 
                 @pl.when(before == count - 1)
@@ -382,7 +382,7 @@
     bf16 = jnp.bfloat16
     spread_sems = sems(count) + sems(count)
     reach_sems = sems(count) + sems(count)
-    buffers = [pltpu.VMEM((count, part, block), jnp.float32) for part in [rows // vp_size * groups]] * 3
+    buffers = [pltpu.VMEM((count, part, block), bf16) for part in [rows // vp_size * groups]] * 3
 
     up_own, down_own = up_weight[0], down_weight[0]
     half = up_own.shape[1] // 2
@@ -423,17 +423,17 @@
     )
     for s in range(2):
         gain, up, down = section_of(s)
-        hidden = jnp.dot(full, up, preferred_element_type=jnp.float32)
+        hidden = jnp.dot(full, up, preferred_element_type=jnp.float32).astype(bf16)
         piece = hidden.shape[0] // (2 * PIECES)
         active = call(
             chain_kernel,
             "chain",
             1,
             jax.ShapeDtypeStruct(hidden.shape, bf16),
-            [pltpu.VMEM((2, PIECES, piece, half), jnp.float32)] * 2 + sems(2, PIECES) + sems(2, PIECES),
+            [pltpu.VMEM((2, PIECES, piece, half), bf16)] * 2 + sems(2, PIECES) + sems(2, PIECES),
             hidden,
         )
-        out = jnp.dot(active, down, preferred_element_type=jnp.float32)
+        out = jnp.dot(active, down, preferred_element_type=jnp.float32).astype(bf16)
         if s == 0:
             gain = section_of(1)[0]
             blocks, full = call(

time: 407 us -> 315 us (0.77)
  Pallas kernels: 345 us -> 256 us
    pallas_call x6, Pallas kernels: 345 us -> 256 us  [call(): pl.pallas_call(kernel, name=name, out_shape=outs, in_specs=[spec] * len(a...]
  transfers between devices with their start and end apart: 3 -> 3, of which waited for: 0 -> 0; matrix products, arithmetic and copies ran while one was open for 3% -> 4% of each run, Pallas kernels for 32% -> 31%
where the time goes in v1:
time: 315 us
  Pallas kernels  256 us (81%)
  matrix products  41.7 us (13%)
  other arithmetic  9.22 us (3%)
  local copies, waits for them, and re-layouts  6.21 us (2%)
    pallas_call x6, Pallas kernels, call(): pl.pallas_call(kernel, name=name, out_shape=outs, in_specs=[spec] * len(a...  256 us
    dot_general x1, matrix products, shards(): lax.dot_general(normed_final, unembedding, (((1,), (1,)), ((), ())), pref...  17.5 us
    dot_general x2, matrix products, shards(): hidden = jnp.dot(full, up, preferred_element_type=jnp.float32).astype(bf16)  12.1 us
    dot_general x2, matrix products, shards(): out = jnp.dot(active, down, preferred_element_type=jnp.float32).astype(bf16)  12.1 us
  transfers between devices with their start and end apart: 3, of which 0 were waited for; matrix products, arithmetic and copies ran while one was open for 4% of the time, Pallas kernels for 31%

profile of v1, /device:TPU:0, one launch (start us, length us, event | category | flops | bytes accessed | tf_op | source)
XLA Modules:
  0.0 314.8 jit_solution(13346578848255693343)
XLA Ops:
  0.6 0.0 copy-start
  0.6 0.6 collective-permute-start
  1.2 0.0 copy-start.2
  1.2 3.1 dynamic-slice_bitcast_fusion.1
  4.3 0.0 copy-start.7
  4.3 0.1 collective-permute-start.1
  4.4 0.0 copy-done.2
  4.4 1.4 dynamic-slice_bitcast_fusion
  5.8 0.5 collective-permute-start.2
  6.3 0.0 copy-done
  6.3 0.7 constant_dynamic-slice_fusion.x_ref
  7.0 0.0 copy-done.7
  7.0 0.0 copy-done.4
  7.0 0.1 convert_reduce_fusion
  7.2 0.0 copy-done.8
  7.2 0.1 slice.23
  7.3 0.1 slice.24
  7.4 0.1 sub.59
  7.4 0.6 pad.9.counts_ref
  8.0 0.0 collective-permute-done
  8.0 0.0 copy-done.3
  8.0 0.6 broadcast_select_fusion.gain_ref
  8.7 28.2 %first.1 = (bf16[128,1024]{1,0:T(8,128)(2,1)}, bf16[1024,1024]{1,0:T(8,128)(2,1)}) custom-call(bf16[32,4096]{1,0:T(8,128)(2,1)} %constant_dynamic-slice_fusion.x_ref, f32[1,4096]{1,0:T(1,128)} %broadcast_select_fusion.gain_ref), custom_call_target="tpu_custom_call" | custom-call | tf_op jit(solution)/shard_map/first/pallas_call | solution.py:343
  36.9 0.6 broadcast_select_fusion.1.gain_ref
  37.5 0.0 collective-permute-done.1
  37.5 5.8 %fusion.7.h_ref = bf16[1024,896]{1,0:T(8,128)(2,1)} fusion(bf16[1024,1024]{1,0:T(8,128)(2,1)} %get-tuple-element.9, bf16[1024,896]{1,0:T(8,128)(2,1)} %collective-permute-done.1, pred[]{:T(512)S(6)} %eq.46, bf16[1,1024,1792]{2,1,0:T(8,128)(2,1)} %param.11, s32[]{:T(128)S(6)} %select_n.74), kind=kOutput, calls=%fused_computation.18 | convolution fusion | flops 1880883200 | bytes 7602181 | tf_op jit(solution)/shard_map/dot_general | solution.py:426
  43.3 69.4 %chain.2 = bf16[1024,896]{1,0:T(8,128)(2,1)} custom-call(bf16[1024,896]{1,0:T(8,128)(2,1)} %fusion.7.h_ref), custom_call_target="tpu_custom_call" | custom-call | tf_op jit(solution)/shard_map/chain/pallas_call | solution.py:343
  112.6 0.0 collective-permute-done.2
  112.7 5.7 %convolution_convert_fusion.1.part_ref = bf16[1024,1024]{1,0:T(8,128)(2,1)} fusion(bf16[1024,896]{1,0:T(8,128)(2,1)} %chain.2, bf16[896,1024]{1,0:T(8,128)(2,1)} %collective-permute-done.2, pred[]{:T(512)S(6)} %eq.46, bf16[1,1792,1024]{2,1,0:T(8,128)(2,1)} %param.12, s32[]{:T(128)S(6)} %select_n.74), kind=kOutput, calls=%fused_computation.4 | convolution fusion | flops 1881014272 | bytes 7602181 | tf_op jit(solution)/shard_map/dot_general | solution.py:436
  118.4 39.6 %middle.1 = (bf16[128,1024]{1,0:T(8,128)(2,1)}, bf16[1024,1024]{1,0:T(8,128)(2,1)}) custom-call(bf16[1024,1024]{1,0:T(8,128)(2,1)} %convolution_convert_fusion.1.part_ref, bf16[128,1024]{1,0:T(8,128)(2,1)} %get-tuple-element.10.resid_ref, f32[1,1024]{1,0:T(1,128)} %broadcast_select_fusion.1.gain_ref), custom_call_target="tpu_custom_call" | custom-call | tf_op jit(solution)/shard_map/middle/pallas_call | solution.py:343
  158.0 6.3 %fusion.6.h_ref = bf16[1024,896]{1,0:T(8,128)(2,1)} fusion(bf16[1024,1024]{1,0:T(8,128)(2,1)} %get-tuple-element.11, bf16[1024,896]{1,0:T(8,128)(2,1)} %collective-permute-done.1, pred[]{:T(512)S(6)} %eq.47, bf16[1,1024,1792]{2,1,0:T(8,128)(2,1)} %param.11, s32[]{:T(128)S(6)} %select_n.74), kind=kOutput, calls=%fused_computation.17 | convolution fusion | flops 1880883200 | bytes 7602181 | tf_op jit(solution)/shard_map/dot_general | solution.py:426
  164.3 66.5 %chain.3 = bf16[1024,896]{1,0:T(8,128)(2,1)} custom-call(bf16[1024,896]{1,0:T(8,128)(2,1)} %fusion.6.h_ref), custom_call_target="tpu_custom_call" | custom-call | tf_op jit(solution)/shard_map/chain/pallas_call | solution.py:343
  230.8 6.3 %convolution_convert_fusion.part_ref = bf16[1024,1024]{1,0:T(8,128)(2,1)} fusion(bf16[1024,896]{1,0:T(8,128)(2,1)} %chain.3, bf16[896,1024]{1,0:T(8,128)(2,1)} %collective-permute-done.2, pred[]{:T(512)S(6)} %eq.47, bf16[1,1792,1024]{2,1,0:T(8,128)(2,1)} %param.12, s32[]{:T(128)S(6)} %select_n.74), kind=kOutput, calls=%fused_computation.3 | convolution fusion | flops 1881014272 | bytes 7602181 | tf_op jit(solution)/shard_map/dot_general | solution.py:436
  237.1 40.7 %last.1 = bf16[256,4096]{1,0:T(8,128)(2,1)} custom-call(bf16[1024,1024]{1,0:T(8,128)(2,1)} %convolution_convert_fusion.part_ref, bf16[128,1024]{1,0:T(8,128)(2,1)} %get-tuple-element.12.resid_ref, f32[1,4096]{1,0:T(1,128)} %bitcast.62), custom_call_target="tpu_custom_call" | custom-call | tf_op jit(solution)/shard_map/last/pallas_call | solution.py:343
  277.8 17.5 %fusion.24 = (f32[256]{0:T(256)S(1)}, f32[256,4096]{1,0:T(8,128)}) fusion(bf16[256,4096]{1,0:T(8,128)(2,1)} %last.1, bf16[4096,4096]{1,0:T(8,128)(2,1)} %param.15), kind=kOutput, calls=%fused_computation.56 | convolution fusion | flops 8590983168 | bytes 39846912 | tf_op jit(solution)/shard_map/dot_general | solution.py:471
  295.4 3.5 %exponential_reduce_fusion = (f32[256]{0:T(256)S(1)}, f32[256]{0:T(256)S(1)}) fusion(f32[256,4096]{1,0:T(8,128)} %get-tuple-element.26, f32[256]{0:T(256)S(1)} %get-tuple-element.25, s32[256]{0:T(256)S(1)} %sub.59), kind=kLoop, calls=%fused_computation.2 | loop fusion | flops 5242368 | bytes 4198400 | tf_op jit(solution)/shard_map/reduce_sum | solution.py:479
  298.8 0.6 select_maximum_fusion.stats_ref
  299.4 11.5 %stats.1 = (f32[64,256]{1,0:T(8,128)}, f32[8,128]{1,0:T(8,128)}) custom-call(f32[8,256]{1,0:T(8,128)} %select_maximum_fusion.stats_ref, f32[8,128]{1,0:T(8,128)} %pad.9.counts_ref), custom_call_target="tpu_custom_call" | custom-call | tf_op jit(solution)/shard_map/stats/pallas_call | solution.py:343
  310.9 1.0 slice_reduce_fusion
  311.9 0.1 sub.64
  312.0 0.0 copy-done.6
  312.0 0.1 multiply_reduce_fusion
  312.2 1.2 bitcast_divide_fusion.2
  313.4 0.7 fusion.23
  314.1 0.2 fusion.21
  314.3 0.5 add_multiply_fusion
  314.8 0.0 copy-done.5
  314.8 0.0 copy-done.1
  (9 shorter events, 0.0 us)
Async XLA Ops:
  0.6 5.7 %copy-start = (bf16[4,64,4096]{2,1,0:T(8,128)(2,1)S(1)}, bf16[4,64,4096]{2,1,0:T(8,128)(2,1)}, u32[]{:S(2)}) copy-start(bf16[4,64,4096]{2,1,0:T(8,128)(2,1)} %param.10) | copy-start | bytes 6291460
  0.6 7.4 %collective-permute-start = (f32[1,4096]{1,0:T(1,128)}, f32[1,4096]{1,0:T(1,128)S(1)}, u32[]{:S(2)}, u32[]{:S(2)}) collective-permute-start(f32[1,4096]{1,0:T(1,128)} %param.13), channel_id=1, source_target_pairs={{0,16},{16,0},{1,17},{17,1},{2,18},{18,2},{3,19},{19,3},{4,20},{20... | collective-permute-start | bytes 49160 | tf_op jit(solution)/shard_map/ppermute | solution.py:392
  1.2 3.2 %copy-start.2 = (bf16[1,1792,1024]{2,1,0:T(8,128)(2,1)S(1)}, bf16[1,1792,1024]{2,1,0:T(8,128)(2,1)}, u32[]{:S(2)}) copy-start(bf16[1,1792,1024]{2,1,0:T(8,128)(2,1)} %param.12) | copy-start | bytes 11010052
  4.3 2.7 copy-start.7
  4.3 2.7 copy-start.4
  4.3 2.8 copy-start.8
  4.3 3.7 %copy-start.3 = (f32[1,4096]{1,0:T(1,128)S(1)}, f32[1,4096]{1,0:T(1,128)}, u32[]{:S(2)}) copy-start(f32[1,4096]{1,0:T(1,128)} %param.13) | copy-start | bytes 49156
  4.3 33.1 %collective-permute-start.1 = (bf16[1024,896]{1,0:T(8,128)(2,1)}, bf16[1024,896]{1,0:T(8,128)(2,1)}, u32[]{:S(2)}, u32[]{:S(2)}) collective-permute-start(bf16[1024,896]{1,0:T(8,128)(2,1)} %dynamic-slice_bitcast_fusion.1), channel_id=1, source_target_pairs={{0,16},{16,0},{1,17},{17,1},{2,18},{18,2},{3,19},{19,3},{4,20},{20... | collective-permute-start | bytes 5505032 | tf_op jit(solution)/shard_map/ppermute | solution.py:393
  5.8 106.8 %collective-permute-start.2 = (bf16[896,1024]{1,0:T(8,128)(2,1)}, bf16[896,1024]{1,0:T(8,128)(2,1)}, u32[]{:S(2)}, u32[]{:S(2)}) collective-permute-start(bf16[896,1024]{1,0:T(8,128)(2,1)} %dynamic-slice_bitcast_fusion), channel_id=1, source_target_pairs={{0,16},{16,0},{1,17},{17,1},{2,18},{18,2},{3,19},{19,3},{4,20},{20... | collective-permute-start | bytes 5505032 | tf_op jit(solution)/shard_map/ppermute | solution.py:394
  295.4 19.5 %copy-start.1 = (bf16[4,64,4096]{2,1,0:T(8,128)(2,1)S(1)}, bf16[4,64,4096]{2,1,0:T(8,128)(2,1)}, u32[]{:S(2)}) copy-start(bf16[4,64,4096]{2,1,0:T(8,128)(2,1)} %param.10) | copy-start | bytes 6291460
  295.4 16.7 %copy-start.6 = (f32[4,64]{1,0:T(4,128)S(1)}, f32[4,64]{1,0:T(4,128)}, u32[]{:S(2)}) copy-start(f32[4,64]{1,0:T(4,128)} %param.18) | copy-start | bytes 3076
  312.0 2.8 copy-start.5

commit v2 on v1

v2 whole, which is shorter than its diff:
```python
import functools
import jax
import jax.numpy as jnp
from jax import lax
from jax.experimental import pallas as pl
from jax.experimental.pallas import tpu as pltpu
from jax.sharding import PartitionSpec as P

SEQ_MB = 1

epsilon = 1e-05
ipo_tau = 0.5
VP = ("pipe", "mp")
MESH = pl.DeviceIdType.MESH
BATCHES = 4
PIECES = 4
HOP = 2
STEP = 2


def remote(src, dst, send_sem, recv_sem, target):
    return pltpu.make_async_remote_copy(
        src_ref=src,
        dst_ref=dst,
        send_sem=send_sem,
        recv_sem=recv_sem,
        device_id=target,
        device_id_type=MESH,
    )


def greet(axes):
    barrier = pltpu.get_barrier_semaphore()
    total = 0
    for axis in axes:
        size = lax.axis_size(axis)
        here = lax.axis_index(axis)
        for k in range(1, size):
            pl.semaphore_signal(
                barrier, inc=1, device_id={axis: lax.rem(here + k, size)}, device_id_type=MESH
            )
        total += size - 1
    pl.semaphore_wait(barrier, total)


def chunk_rows(index, size):
    return pl.ds(pl.multiple_of(index * size, 8), size)


def spread(full, size, mp_sems, pipe_sems):
    (mp_send, mp_recv), (pipe_send, pipe_recv) = mp_sems, pipe_sems
    count = lax.axis_size("mp")
    m, p = lax.axis_index("mp"), lax.axis_index("pipe")

    def to_mp(k, owner):
        rows = full.at[chunk_rows(p * count + owner, size)]
        return remote(rows, rows, mp_send.at[k], mp_recv.at[k], {"mp": lax.rem(m + k, count)})

    def to_pipe(k, pipe):
        rows = full.at[chunk_rows(pipe * count + lax.rem(m - k + count, count), size)]
        return remote(rows, rows, pipe_send.at[k], pipe_recv.at[k], {"pipe": 1 - p})

    for k in range(1, count):
        to_mp(k, m).start()
    to_pipe(0, p).start()
    for k in range(1, count):
        to_mp(k, lax.rem(m - k + count, count)).wait_recv()
        to_pipe(k, p).start()
    for k in range(count):
        to_pipe(k, 1 - p).wait_recv()
    for k in range(1, count):
        to_mp(k, m).wait_send()
    for k in range(count):
        to_pipe(k, p).wait_send()


def share_sum(slots, send, recv):
    count = lax.axis_size("dp")
    d = lax.axis_index("dp")

    def hop(k):
        return remote(
            slots.at[0], slots.at[k], send.at[k], recv.at[k], {"dp": lax.rem(d + k, count)}
        )

    for k in range(1, count):
        hop(k).start()
    total = slots[0]
    for k in range(1, count):
        hop(k).wait_recv()
        total = total + slots[k]
    for k in range(1, count):
        hop(k).wait_send()
    return total


def stats_kernel(stats_ref, counts_ref, full_ref, total_ref, slots, qs, qr, ms, mr, ps, pr):
    v = lax.axis_index(("pipe", "mp"))
    size = stats_ref.shape[0]
    greet(("dp", "mp", "pipe"))
    slots[0] = counts_ref[...]
    full_ref[chunk_rows(v, size), :] = stats_ref[...]
    total_ref[...] = share_sum(slots, qs, qr)
    spread(full_ref, size, (ms, mr), (ps, pr))


def meet():
    barrier = pltpu.get_barrier_semaphore()
    n, count = lax.axis_size("dp"), lax.axis_size("mp")
    d, m, p = lax.axis_index("dp"), lax.axis_index("mp"), lax.axis_index("pipe")
    for k in range(1, n):
        pl.semaphore_signal(
            barrier, inc=1, device_id={"dp": lax.rem(d + k, n)}, device_id_type=MESH
        )
    for k in range(1, count):
        pl.semaphore_signal(
            barrier, inc=1, device_id={"mp": lax.rem(m + k, count)}, device_id_type=MESH
        )
    for k in range(count):
        pl.semaphore_signal(
            barrier,
            inc=1,
            device_id={"mp": lax.rem(m + k, count), "pipe": 1 - p},
            device_id_type=MESH,
        )
    pl.semaphore_wait(barrier, n - 1 + count - 1 + count)


def relay_kernel(
    x_hbm, up_hbm, down_hbm, layer_gain, final_gain, full_ref,
    up, down, xs, normed, xin, hid, act, ext, outs, rs, resid, nxt, slots, fin,
    load, go, ns, nr, xs_s, xs_r, gs, gr, ins, inr, exr, bs, br, rss, rsr, ds, dr, qs, qr,
    hs, hr, fs, fr, es, er,
):
    n, count = lax.axis_size("dp"), lax.axis_size("mp")
    d, m, p = lax.axis_index("dp"), lax.axis_index("mp"), lax.axis_index("pipe")
    length, width = x_hbm.shape
    block, ff = up.shape
    part = length // count
    sub = part // BATCHES
    own_rows = sub * n
    batch = own_rows * count
    half = batch // 2
    piece = half // PIECES
    total = BATCHES * PIECES
    f32 = jnp.float32

    def rows(start, size):
        return pl.ds(pl.multiple_of(start, 16), size)

    def columns(owner):
        return pl.ds(pl.multiple_of(owner * block, 128), block)

    loads = [
        pltpu.make_async_copy(x_hbm.at[rows(m * part, part)], xs, load.at[0]),
        pltpu.make_async_copy(up_hbm, up, load.at[1]),
        pltpu.make_async_copy(down_hbm, down, load.at[2]),
    ]
    for copy in loads:
        copy.start()
    meet()
    loads[0].wait()

    def first_hop(b, k, owner):
        to = lax.rem(d + k, n)
        return remote(
            normed.at[rows(b * sub, sub), columns(to)],
            xin.at[rows(b * batch + (m * n + owner) * sub, sub)],
            ns.at[b, k],
            nr.at[b, k],
            {"dp": to},
        )

    def plain_hop(b, k, owner):
        to = lax.rem(d + k, n)
        return remote(
            xs.at[rows(b * sub, sub), columns(to)],
            resid.at[rows(b * own_rows + owner * sub, sub)],
            xs_s.at[b, k],
            xs_r.at[b, k],
            {"dp": to},
        )

    def share(b, k, owner):
        slab = xin.at[rows(b * batch + owner * own_rows, own_rows)]
        return remote(slab, slab, gs.at[b, k], gr.at[b, k], {"mp": lax.rem(m + k, count)})

    def scatter(b, k):
        to = lax.rem(m + k, count)
        return remote(
            outs.at[rows(b * batch + to * own_rows, own_rows)],
            rs.at[rows((b * count + k) * own_rows, own_rows)],
            rss.at[b, k],
            rsr.at[b, k],
            {"mp": to, "pipe": 1 - p},
        )

    def hand_over(b):
        slab = rows(b * own_rows, own_rows)
        return remote(nxt.at[slab], resid.at[slab], ds.at[b], dr.at[b], {"pipe": 1 - p})

    def square(b, k):
        return remote(
            slots.at[b, 0], slots.at[b, k], qs.at[b, k], qr.at[b, k], {"dp": lax.rem(d + k, n)}
        )

    def last_hop(b, k, owner):
        to = lax.rem(d + k, n)
        return remote(
            nxt.at[rows(b * own_rows + to * sub, sub)],
            fin.at[b, owner],
            hs.at[b, k],
            hr.at[b, k],
            {"dp": to},
        )

    def spot(b, owner):
        return full_ref.at[rows(owner * part + b * sub, sub)]

    def full_share(b, k, owner):
        return remote(
            spot(b, owner), spot(b, owner), fs.at[b, k], fr.at[b, k], {"mp": lax.rem(m + k, count)}
        )

    def full_pass(b, k):
        owner = lax.rem(m - k + count, count)
        return remote(
            spot(b, owner), spot(b, owner), es.at[b, k], er.at[b, k], {"pipe": 1 - p}
        )

    def before(k):
        return lax.rem(d - k + n, n)

    def beside(k):
        return lax.rem(m - k + count, count)

    @pl.when(p == 0)
    def _():
        wide = xs[...].astype(f32)
        scale = lax.rsqrt(jnp.mean(wide * wide, axis=-1, keepdims=True) + epsilon)
        normed[...] = (wide * scale * layer_gain[...]).astype(normed.dtype)
        for b in range(BATCHES):
            for k in range(1, n):
                first_hop(b, k, d).start()
        for b in range(BATCHES):
            xin[rows(b * batch + (m * n + d) * sub, sub), :] = normed[
                b * sub : (b + 1) * sub, columns(d)
            ]
        for b in range(BATCHES):
            for k in range(1, n):
                first_hop(b, k, before(k)).wait_recv()
            for k in range(1, count):
                share(b, k, m).start()
        pl.semaphore_signal(go, inc=1, device_id={"pipe": 1 - p}, device_id_type=MESH)

    @pl.when(p == 1)
    def _():
        pl.semaphore_wait(go, 1)
        for b in range(BATCHES):
            for k in range(1, n):
                plain_hop(b, k, d).start()
            resid[rows(b * own_rows + d * sub, sub), :] = xs[b * sub : (b + 1) * sub, columns(d)]

    loads[1].wait()
    loads[2].wait()

    def enter(b):
        for k in range(1, count):
            share(b, k, beside(k)).wait_recv()
        where = rows(b * batch, batch)
        states = xin[where, :]
        step = 256
        for j in range(0, ff, step):
            hid[where, j : j + step] = jnp.dot(
                states, up[:, j : j + step], preferred_element_type=f32
            ).astype(hid.dtype)

    def leave(b):
        where = rows(b * batch, batch)
        states = act[where, :]
        step = min(block, 256)
        for j in range(0, block, step):
            outs[where, j : j + step] = jnp.dot(
                states, down[:, j : j + step], preferred_element_type=f32
            ).astype(outs.dtype)
        for k in (*range(1, count), 0):
            scatter(b, k).start()

    def add_up(b):
        for k in range(count):
            scatter(b, k).wait_recv()
        slab = rows(b * own_rows, own_rows)
        value = resid[slab, :].astype(f32)
        for k in range(count):
            value = value + rs[rows((b * count + k) * own_rows, own_rows), :].astype(f32)
        value = value.astype(nxt.dtype)
        nxt[slab, :] = value
        return value.astype(f32)

    def settle(b):
        for k in range(1, n):
            plain_hop(b, k, before(k)).wait_recv()
        wide = add_up(b)
        sums = jnp.sum(wide * wide, axis=1, keepdims=True)
        slots[b, 0] = jnp.broadcast_to(sums, (own_rows, 128))
        for k in range(1, n):
            square(b, k).start()
        hand_over(b).start()

    def renew(b):
        sums = slots[b, 0]
        for k in range(1, n):
            square(b, k).wait_recv()
            sums = sums + slots[b, k]
        scale = lax.rsqrt(sums[:, :1] / width + epsilon)
        wide = nxt[rows(b * own_rows, own_rows), :].astype(f32)
        gain = layer_gain[:, columns(d)]
        xin[rows(b * batch + m * own_rows, own_rows), :] = (wide * scale * gain).astype(xin.dtype)
        for k in range(1, count):
            share(b, k, m).start()

    def span(way, c):
        b, k = lax.div(c, PIECES), lax.rem(c, PIECES)
        return rows(b * batch + way * half + k * piece, piece)

    def inner(way, c, to, into, sem):
        return remote(hid.at[span(way, c)], into, ins.at[way, c], sem.at[way, c], {"dp": to})

    def to_act(way, c, to):
        return inner(way, c, to, act.at[span(way, c)], inr)

    def to_ext(way, c, to):
        return inner(way, c, to, ext.at[rows(c * piece, piece)], exr)

    def outer(way, c, side):
        where = act.at[span(way, c)]
        to = d - 1 if side == 0 else d + 1
        return remote(where, where, bs.at[way, c, side], br.at[way, c], {"dp": to})

    offset = 2 * STEP + 1
    deep = HOP * (n // 2)
    ticks = offset + total + 2 * deep

    def tick(t, carry):
        now = t - offset
        for way in range(2):
            owner = n // 2 - way
            left, right = d < owner, d > owner
            hops = jnp.where(left, d, n - 1 - d)
            c = now - HOP * hops

            @pl.when((d != owner) & (c >= 0) & (c < total))
            def _():
                here = span(way, c)

                @pl.when(hops > 0)
                def _():
                    to_act(way, c, d).wait_recv()
                    for j in range(0, ff, 256):
                        cut = slice(j, j + 256)
                        hid[here, cut] = (
                            hid[here, cut].astype(f32) + act[here, cut].astype(f32)
                        ).astype(hid.dtype)

                @pl.when(left)
                def _():
                    to_act(way, c, d + 1).start()

                @pl.when(right & (d - 1 > owner))
                def _():
                    to_act(way, c, d - 1).start()

                @pl.when(right & (d - 1 == owner))
                def _():
                    to_ext(way, c, d - 1).start()

        for way in range(2):
            owner = n // 2 - way
            c = now - deep

            @pl.when((d == owner) & (c >= 0) & (c < total))
            def _():
                here = span(way, c)
                there = rows(c * piece, piece)
                if owner > 0:
                    to_act(way, c, d).wait_recv()
                if owner < n - 1:
                    to_ext(way, c, d).wait_recv()
                for j in range(0, ff, 256):
                    cut = slice(j, j + 256)
                    value = hid[here, cut].astype(f32)
                    if owner > 0:
                        value = value + act[here, cut].astype(f32)
                    if owner < n - 1:
                        value = value + ext[there, cut].astype(f32)
                    act[here, cut] = (value / (1.0 + jnp.exp(-value))).astype(act.dtype)
                if owner > 0:
                    outer(way, c, 0).start()
                if owner < n - 1:
                    outer(way, c, 1).start()

        for way in range(2):
            owner = n // 2 - way
            left, right = d < owner, d > owner
            away = jnp.where(left, owner - d, d - owner)
            c = now - deep - HOP * away

            @pl.when((d != owner) & (c >= 0) & (c < total))
            def _():
                outer(way, c, 0).wait_recv()

                @pl.when(left & (d > 0))
                def _():
                    outer(way, c, 0).start()

                @pl.when(right & (d < n - 1))
                def _():
                    outer(way, c, 1).start()

        b = lax.div(now + 1, PIECES)

        @pl.when((now + 1 >= 0) & (lax.rem(now + 1, PIECES) == 0) & (b < BATCHES))
        def _():
            enter(b)

        done = now - (PIECES - 1) - 2 * deep
        q = lax.div(done, PIECES)

        @pl.when((done >= 0) & (lax.rem(done, PIECES) == 0) & (q < BATCHES))
        def _():
            leave(q)

        late = now + 1 + STEP
        e = lax.div(late, PIECES)

        @pl.when((p == 1) & (late >= 0) & (lax.rem(late, PIECES) == 0) & (e < BATCHES))
        def _():
            renew(e)

        early = now + 1 + 2 * STEP
        a = lax.div(early, PIECES)

        @pl.when((p == 1) & (lax.rem(early, PIECES) == 0) & (a < BATCHES))
        def _():
            settle(a)

        return carry

    lax.fori_loop(0, ticks, tick, 0)

    @pl.when(p == 0)
    def _():
        def finish(b, carry):
            hand_over(b).wait_recv()
            add_up(b)
            for k in range(1, n):
                last_hop(b, k, d).start()
            fin[b, d] = nxt[rows(b * own_rows + d * sub, sub), :]
            for k in range(1, n):
                last_hop(b, k, before(k)).wait_recv()
            sums = 0.0
            for g in range(n):
                wide = fin[b, g].astype(f32)
                sums = sums + jnp.sum(wide * wide, axis=1, keepdims=True)
            scale = lax.rsqrt(sums / width + epsilon)
            for g in range(n):
                cut = slice(g * block, (g + 1) * block)
                full_ref[rows(m * part + b * sub, sub), cut] = (
                    fin[b, g].astype(f32) * scale * final_gain[:, cut]
                ).astype(full_ref.dtype)
            for k in range(1, count):
                full_share(b, k, m).start()
            full_pass(b, 0).start()
            for k in range(1, count):
                full_share(b, k, beside(k)).wait_recv()
                full_pass(b, k).start()
            return carry

        lax.fori_loop(0, BATCHES, finish, 0)

    @pl.when(p == 1)
    def _():
        def finish(b, carry):
            for k in range(count):
                full_pass(b, k).wait_recv()
            return carry

        lax.fori_loop(0, BATCHES, finish, 0)

    def drain(b, carry):
        for k in range(1, count):
            share(b, k, m).wait_send()
        for k in range(count):
            scatter(b, k).wait_send()

        @pl.when(p == 0)
        def _():
            for k in range(1, n):
                first_hop(b, k, d).wait_send()
                last_hop(b, k, d).wait_send()
            for k in range(1, count):
                full_share(b, k, m).wait_send()
            for k in range(count):
                full_pass(b, k).wait_send()

        @pl.when(p == 1)
        def _():
            for k in range(1, n):
                plain_hop(b, k, d).wait_send()
                square(b, k).wait_send()
            hand_over(b).wait_send()

        return carry

    lax.fori_loop(0, BATCHES, drain, 0)

    def drain_pieces(c, carry):
        for way in range(2):
            owner = n // 2 - way

            @pl.when(d != owner)
            def _():
                to_act(way, c, d).wait_send()

            @pl.when((d <= owner) & (d > 0))
            def _():
                outer(way, c, 0).wait_send()

            @pl.when((d >= owner) & (d < n - 1))
            def _():
                outer(way, c, 1).wait_send()

        return carry

    lax.fori_loop(0, total, drain_pieces, 0)


def call(kernel, name, ident, outs, scratch, *args):
    spec = pl.BlockSpec(memory_space=pltpu.VMEM)
    return pl.pallas_call(
        kernel,
        name=name,
        out_shape=outs,
        in_specs=[spec] * len(args),
        out_specs=jax.tree.map(lambda _: spec, outs),
        scratch_shapes=scratch,
        compiler_params=pltpu.CompilerParams(collective_id=ident, has_side_effects=True),
    )(*args)


def sems(*shape):
    return [pltpu.SemaphoreType.DMA(shape)] * 2


def shards(
    hidden_states,
    up_weight,
    down_weight,
    layer_gain,
    final_gain,
    unembedding,
    target_ids,
    response_masks,
    anchor_logps,
    pairing,
):
    seq_count, length, model_width = hidden_states.shape
    groups = lax.axis_size("dp")
    vp_size = lax.axis_size("pipe") * lax.axis_size("mp")
    vp_index = lax.axis_index(VP)
    rows = seq_count * length
    block = model_width // groups
    ff = up_weight.shape[2]
    mask_values = response_masks.astype(jnp.float32)
    local_counts = jnp.sum(mask_values, axis=1)
    count = lax.axis_size("mp")
    bf16 = jnp.bfloat16
    spread_sems = sems(count) + sems(count)
    part = rows // count
    own_rows = part * groups
    all_rows = rows * groups
    steps = BATCHES * PIECES
    anyspec = pl.BlockSpec(memory_space=pl.ANY)
    spec = pl.BlockSpec(memory_space=pltpu.VMEM)
    dma = pltpu.SemaphoreType.DMA
    normed_final = pl.pallas_call(
        relay_kernel,
        name="relay",
        out_shape=jax.ShapeDtypeStruct((rows, model_width), bf16),
        in_specs=[anyspec, anyspec, anyspec, spec, spec],
        out_specs=spec,
        scratch_shapes=[
            pltpu.VMEM((block, ff), bf16),
            pltpu.VMEM((ff, block), bf16),
            pltpu.VMEM((part, model_width), bf16),
            pltpu.VMEM((part, model_width), bf16),
            pltpu.VMEM((all_rows, block), bf16),
            pltpu.VMEM((all_rows, ff), bf16),
            pltpu.VMEM((all_rows, ff), bf16),
            pltpu.VMEM((all_rows // 2, ff), bf16),
            pltpu.VMEM((all_rows, block), bf16),
            pltpu.VMEM((all_rows, block), bf16),
            pltpu.VMEM((own_rows, block), bf16),
            pltpu.VMEM((own_rows, block), bf16),
            pltpu.VMEM((BATCHES, groups, own_rows // BATCHES, 128), jnp.float32),
            pltpu.VMEM((BATCHES, groups, part // BATCHES, block), bf16),
            dma((3,)),
            pltpu.SemaphoreType.REGULAR,
        ]
        + sems(BATCHES, groups)
        + sems(BATCHES, groups)
        + sems(BATCHES, count)
        + [dma((2, steps))] * 3
        + [dma((2, steps, 2)), dma((2, steps))]
        + sems(BATCHES, count)
        + sems(BATCHES)
        + sems(BATCHES, groups)
        + sems(BATCHES, groups)
        + sems(BATCHES, count)
        + sems(BATCHES, count),
        compiler_params=pltpu.CompilerParams(
            collective_id=0, has_side_effects=True, vmem_limit_bytes=62 * 1024 * 1024
        ),
    )(
        hidden_states.reshape(rows, model_width),
        up_weight[0],
        down_weight[0],
        layer_gain,
        final_gain[None],
    )
    logits = lax.dot_general(
        normed_final, unembedding, (((1,), (1,)), ((), ())), preferred_element_type=jnp.float32
    )
    vocab_start = vp_index * unembedding.shape[0]
    local_ids = target_ids.reshape(-1) - vocab_start
    columns = lax.broadcasted_iota(jnp.int32, logits.shape, 1)
    picked = jnp.sum(jnp.where(columns == local_ids[:, None], logits, 0.0), axis=1)
    local_top = jnp.max(logits, axis=1)
    local_sum = jnp.sum(jnp.exp(logits - local_top[:, None]), axis=1)
    stats = jnp.pad(jnp.stack([local_top, local_sum, picked]), ((0, 5), (0, 0)))
    padded = jnp.pad(local_counts[None], ((0, 7), (0, -seq_count % 128)))
    stats, counts = call(
        stats_kernel,
        "stats",
        1,
        [
            jax.ShapeDtypeStruct((vp_size * 8, rows), jnp.float32),
            jax.ShapeDtypeStruct(padded.shape, jnp.float32),
        ],
        [pltpu.VMEM((groups,) + padded.shape, jnp.float32)] + sems(groups) + spread_sems,
        stats,
        padded,
    )
    stats = stats.reshape(vp_size, 8, rows)
    counts = counts[0, :seq_count]
    top_value = jnp.max(stats[:, 0], axis=0)
    exp_total = jnp.sum(stats[:, 1] * jnp.exp(stats[:, 0] - top_value), axis=0)
    picked_all = jnp.sum(stats[:, 2], axis=0)
    token_logps = (picked_all - top_value - jnp.log(exp_total)).reshape(seq_count, length)

    divisor = jnp.repeat(counts / (groups * SEQ_MB), SEQ_MB)
    policy = jnp.sum(mask_values * token_logps, axis=1) / divisor
    anchor = jnp.sum(mask_values * anchor_logps, axis=1) / divisor
    log_gaps = policy - anchor
    positions = jnp.arange(seq_count, dtype=jnp.int32)
    chosen = jnp.sum(
        jnp.where(pairing[0, 0::2][:, None] == positions[None, :], log_gaps[None, :], 0.0), axis=1
    )
    rejected = jnp.sum(
        jnp.where(pairing[0, 1::2][:, None] == positions[None, :], log_gaps[None, :], 0.0), axis=1
    )
    losses = (chosen - rejected - 0.5 / ipo_tau) ** 2
    return (token_logps, policy, losses)


def solution(mesh):
    return jax.shard_map(
        shards,
        mesh=mesh,
        in_specs=(
            P("dp", None, None),
            P("pipe", "dp", "mp"),
            P("pipe", "mp", "dp"),
            P("pipe", None),
            P(),
            P(("pipe", "mp"), None),
            P("dp", None),
            P("dp", None),
            P("dp", None),
            P("dp", None),
        ),
        out_specs=(P("dp", None), P("dp"), P("dp")),
        check_vma=False,
    )
```

time: 315 us -> 195 us (0.62)
  Pallas kernels: 256 us -> 167 us
  matrix products: 41.7 us -> 17.5 us
  local copies, waits for them, and re-layouts: 6.21 us -> 0.97 us
    pallas_call x6 -> x1, Pallas kernels: 256 us -> 11 us  [call(): pl.pallas_call(kernel, name=name, out_shape=outs, in_specs=[spec] * len(a...]
    pallas_call x0 -> x1, Pallas kernels: none -> 156 us  [shards(): pl.pallas_call(relay_kernel, name='relay', out_shape=jax.ShapeDtypeStruct...]
    dot_general x4 -> x0, matrix products: 24.2 us -> none  [the longest x2 12.1 us: shards(): hidden = jnp.dot(full, up, preferred_element_type=jnp.float32).astype(bf16)]
    dynamic_slice x3 -> x0, local copies, waits for them, and re-layouts: 5.23 us -> none  [the longest x1 3.11 us: shards(): lax.dynamic_slice_in_dim(up_own, away, half, 1)]
  transfers between devices with their start and end apart: 3 -> 0, of which waited for: 0 -> 0; matrix products, arithmetic and copies ran while one was open for 4% -> 0% of each run, Pallas kernels for 31% -> 0%
where the time goes in v2:
time: 195 us; the launch traced here: 194 us
  Pallas kernels  167 us (86%)
  matrix products  17.5 us (9%)
  other arithmetic  7.85 us (4%)
    pallas_call x1, Pallas kernels, shards(): pl.pallas_call(relay_kernel, name='relay', out_shape=jax.ShapeDtypeStruct...  156 us
    dot_general x1, matrix products, shards(): lax.dot_general(normed_final, unembedding, (((1,), (1,)), ((), ())), pref...  17.5 us
    pallas_call x1, Pallas kernels, call(): pl.pallas_call(kernel, name=name, out_shape=outs, in_specs=[spec] * len(a...  11 us

profile of v2, /device:TPU:0, one launch (start us, length us, event | category | flops | bytes accessed | tf_op | source)
XLA Modules:
  0.0 194.5 jit_solution(447183596826319957)
XLA Ops:
  0.6 156.4 %relay.1 = bf16[256,4096]{1,0:T(8,128)(2,1)} custom-call(bf16[256,4096]{1,0:T(8,128)(2,1)} %bitcast.43, bf16[1024,1792]{1,0:T(8,128)(2,1)} %bitcast.41, bf16[1792,1024]{1,0:T(8,128)(2,1)} %bitcast.42, f32[1,4096]{1,0:T(1,128)} %layer_gain.1, f32[1,4096]{1,0:T(1,128)} %bitcast.44), custom_call_target="tpu_custom_call" | custom-call | tf_op jit(solution)/shard_map/relay/pallas_call | solution.py:586
  157.0 0.0 copy-start.3
  157.0 17.5 %fusion.8 = (f32[256]{0:T(256)S(1)}, f32[256,4096]{1,0:T(8,128)}) fusion(bf16[256,4096]{1,0:T(8,128)(2,1)} %relay.1, bf16[4096,4096]{1,0:T(8,128)(2,1)} %param.15), kind=kOutput, calls=%fused_computation.29 | convolution fusion | flops 8590983168 | bytes 39846912 | tf_op jit(solution)/shard_map/dot_general | solution.py:631
  174.6 0.0 copy-start
  174.6 0.0 copy-start.2
  174.6 0.0 copy-start.4
  174.6 0.0 copy-done.3
  174.6 0.1 sub.55
  174.7 3.3 %exponential_reduce_fusion = (f32[256]{0:T(256)S(1)}, f32[256]{0:T(256)S(1)}) fusion(f32[256,4096]{1,0:T(8,128)} %get-tuple-element.18, f32[256]{0:T(256)S(1)} %get-tuple-element.17, s32[256]{0:T(256)S(1)} %sub.55), kind=kLoop, calls=%fused_computation.2 | loop fusion | flops 5242368 | bytes 4198400 | tf_op jit(solution)/shard_map/reduce_sum | solution.py:639
  178.0 0.6 select_maximum_fusion.stats_ref
  178.6 0.0 copy-done
  178.6 0.1 convert_reduce_fusion
  178.7 0.6 pad.9.counts_ref
  179.3 11.0 %stats.1 = (f32[64,256]{1,0:T(8,128)}, f32[8,128]{1,0:T(8,128)}) custom-call(f32[8,256]{1,0:T(8,128)} %select_maximum_fusion.stats_ref, f32[8,128]{1,0:T(8,128)} %pad.9.counts_ref), custom_call_target="tpu_custom_call" | custom-call | tf_op jit(solution)/shard_map/stats/pallas_call | solution.py:540
  190.4 1.0 slice_reduce_fusion
  191.4 0.1 sub.60
  191.5 0.0 copy-done.2
  191.5 0.0 copy-start.1
  191.5 0.1 multiply_reduce_fusion
  191.6 0.7 fusion.7
  192.3 0.0 copy-done.4
  192.3 0.1 slice.23
  192.4 0.1 slice.24
  192.5 0.2 fusion.5
  192.7 0.5 add_multiply_fusion
  193.3 1.2 bitcast_divide_fusion.2
  194.5 0.0 copy-done.1
  (3 shorter events, 0.0 us)
Async XLA Ops:
  157.0 17.5 %copy-start.3 = (s32[4,64]{1,0:T(4,128)S(1)}, s32[4,64]{1,0:T(4,128)}, u32[]{:S(2)}) copy-start(s32[4,64]{1,0:T(4,128)} %param.16) | copy-start | bytes 3076
  174.6 4.0 %copy-start = (s32[4,64]{1,0:T(4,128)S(1)}, s32[4,64]{1,0:T(4,128)}, u32[]{:S(2)}) copy-start(s32[4,64]{1,0:T(4,128)} %param.17) | copy-start | bytes 3076
  174.6 16.9 %copy-start.2 = (f32[4,64]{1,0:T(4,128)S(1)}, f32[4,64]{1,0:T(4,128)}, u32[]{:S(2)}) copy-start(f32[4,64]{1,0:T(4,128)} %param.18) | copy-start | bytes 3076
  174.6 17.8 %copy-start.4 = (s32[1,4]{1,0:T(1,128)S(1)}, s32[1,4]{1,0:T(1,128)}, u32[]{:S(2)}) copy-start(s32[1,4]{1,0:T(1,128)} %param.19) | copy-start | bytes 52
  191.5 3.0 %copy-start.1 = (f32[4,64]{1,0:T(4,128)}, f32[4,64]{1,0:T(4,128)S(1)}, u32[]{:S(2)}) copy-start(f32[4,64]{1,0:T(4,128)S(1)} %sub.60) | copy-start | bytes 3076

commit v3 on v2

--- a/solution.py
+++ b/solution.py
@@ -1,4 +1,4 @@
-import functools
+import math
 import jax
 import jax.numpy as jnp
 from jax import lax
@@ -10,12 +10,12 @@
 
 epsilon = 1e-05
 ipo_tau = 0.5
-VP = ("pipe", "mp")
 MESH = pl.DeviceIdType.MESH
 BATCHES = 4
 PIECES = 4
 HOP = 2
 STEP = 2
+ROOM = 62 * 1024 * 1024
 
 
 def remote(src, dst, send_sem, recv_sem, target):
@@ -29,81 +29,6 @@
     )
 
 
-def greet(axes):
-    barrier = pltpu.get_barrier_semaphore()
-    total = 0
-    for axis in axes:
-        size = lax.axis_size(axis)
-        here = lax.axis_index(axis)
-        for k in range(1, size):
-            pl.semaphore_signal(
-                barrier, inc=1, device_id={axis: lax.rem(here + k, size)}, device_id_type=MESH
-            )
-        total += size - 1
-    pl.semaphore_wait(barrier, total)
-
-
-def chunk_rows(index, size):
-    return pl.ds(pl.multiple_of(index * size, 8), size)
-
-
-def spread(full, size, mp_sems, pipe_sems):
-    (mp_send, mp_recv), (pipe_send, pipe_recv) = mp_sems, pipe_sems
-    count = lax.axis_size("mp")
-    m, p = lax.axis_index("mp"), lax.axis_index("pipe")
-
-    def to_mp(k, owner):
-        rows = full.at[chunk_rows(p * count + owner, size)]
-        return remote(rows, rows, mp_send.at[k], mp_recv.at[k], {"mp": lax.rem(m + k, count)})
-
-    def to_pipe(k, pipe):
-        rows = full.at[chunk_rows(pipe * count + lax.rem(m - k + count, count), size)]
-        return remote(rows, rows, pipe_send.at[k], pipe_recv.at[k], {"pipe": 1 - p})
-
-    for k in range(1, count):
-        to_mp(k, m).start()
-    to_pipe(0, p).start()
-    for k in range(1, count):
-        to_mp(k, lax.rem(m - k + count, count)).wait_recv()
-        to_pipe(k, p).start()
-    for k in range(count):
-        to_pipe(k, 1 - p).wait_recv()
-    for k in range(1, count):
-        to_mp(k, m).wait_send()
-    for k in range(count):
-        to_pipe(k, p).wait_send()
-
-
-def share_sum(slots, send, recv):
-    count = lax.axis_size("dp")
-    d = lax.axis_index("dp")
-
-    def hop(k):
-        return remote(
-            slots.at[0], slots.at[k], send.at[k], recv.at[k], {"dp": lax.rem(d + k, count)}
-        )
-
-    for k in range(1, count):
-        hop(k).start()
-    total = slots[0]
-    for k in range(1, count):
-        hop(k).wait_recv()
-        total = total + slots[k]
-    for k in range(1, count):
-        hop(k).wait_send()
-    return total
-
-
-def stats_kernel(stats_ref, counts_ref, full_ref, total_ref, slots, qs, qr, ms, mr, ps, pr):
-    v = lax.axis_index(("pipe", "mp"))
-    size = stats_ref.shape[0]
-    greet(("dp", "mp", "pipe"))
-    slots[0] = counts_ref[...]
-    full_ref[chunk_rows(v, size), :] = stats_ref[...]
-    total_ref[...] = share_sum(slots, qs, qr)
-    spread(full_ref, size, (ms, mr), (ps, pr))
-
-
 def meet():
     barrier = pltpu.get_barrier_semaphore()
     n, count = lax.axis_size("dp"), lax.axis_size("mp")
@@ -127,10 +52,10 @@
 
 
 def relay_kernel(
-    x_hbm, up_hbm, down_hbm, layer_gain, final_gain, full_ref,
-    up, down, xs, normed, xin, hid, act, ext, outs, rs, resid, nxt, slots, fin,
+    x_hbm, up_hbm, down_hbm, head_hbm, layer_gain, final_gain, ids_ref, mask_ref, anchor_ref,
+    pairs_ref, token_ref, policy_ref, loss_ref, full_ref, head, stats, tallies, up, down, xs, normed, xin, hid, act, ext, outs, rs, resid, nxt, slots, fin,
     load, go, ns, nr, xs_s, xs_r, gs, gr, ins, inr, exr, bs, br, rss, rsr, ds, dr, qs, qr,
-    hs, hr, fs, fr, es, er,
+    hs, hr, fs, fr, es, er, load_head, ts, tr, vs, vr,
 ):
     n, count = lax.axis_size("dp"), lax.axis_size("mp")
     d, m, p = lax.axis_index("dp"), lax.axis_index("mp"), lax.axis_index("pipe")
@@ -159,6 +84,31 @@
     for copy in loads:
         copy.start()
     meet()
+    seq_count, seq_len = mask_ref.shape
+
+    def flat(ref):
+        return jnp.concatenate([ref[s : s + 1, :] for s in range(seq_count)], axis=1)
+
+    lanes = lax.broadcasted_iota(jnp.int32, (length, 128), 1)
+    member = (lanes == lax.broadcasted_iota(jnp.int32, (length, 128), 0) // seq_len).astype(f32)
+
+    def per_sequence(row):
+        return lax.dot_general(
+            jnp.broadcast_to(row, (8, length)),
+            member,
+            (((1,), (0,)), ((), ())),
+            precision=lax.Precision.HIGHEST,
+            preferred_element_type=f32,
+        )
+
+    mask = flat(mask_ref).astype(f32)
+    tallies[0] = per_sequence(mask)
+
+    def tally(k):
+        return remote(
+            tallies.at[0], tallies.at[k], ts.at[k], tr.at[k], {"dp": lax.rem(d + k, n)}
+        )
+
     loads[0].wait()
 
     def first_hop(b, k, owner):
@@ -261,8 +211,22 @@
                 plain_hop(b, k, d).start()
             resid[rows(b * own_rows + d * sub, sub), :] = xs[b * sub : (b + 1) * sub, columns(d)]
 
+    for k in range(1, n):
+        tally(k).start()
     loads[1].wait()
     loads[2].wait()
+    slots_head, tall, _ = head.shape
+    vocab = head_hbm.shape[0]
+
+    def head_load(j):
+        return pltpu.make_async_copy(
+            head_hbm.at[pl.ds(j * tall, tall)],
+            head.at[j % slots_head],
+            load_head.at[j % slots_head],
+        )
+
+    for j in range(slots_head):
+        head_load(j).start()
 
     def enter(b):
         for k in range(1, count):
@@ -487,6 +451,79 @@
 
         lax.fori_loop(0, BATCHES, finish, 0)
 
+    states = full_ref[...]
+    ids = flat(ids_ref) - (p * count + m) * vocab
+    spots = lax.broadcasted_iota(jnp.int32, (tall, length), 0)
+    top = jnp.full((1, length), -jnp.inf, f32)
+    mass = jnp.zeros((1, length), f32)
+    picked = jnp.zeros((1, length), f32)
+
+    def gauge(j, logits, carry):
+        top, mass, picked = carry
+        peak = jnp.maximum(top, jnp.max(logits, axis=0, keepdims=True))
+        mass = mass * jnp.exp(top - peak) + jnp.sum(jnp.exp(logits - peak), axis=0, keepdims=True)
+        hit = jnp.where(spots == ids - j * tall, logits, 0.0)
+        return peak, mass, picked + jnp.sum(hit, axis=0, keepdims=True)
+
+    carry = top, mass, picked
+    last = None
+    for j in range(vocab // tall):
+        head_load(j).wait()
+        logits = lax.dot_general(
+            head[j % slots_head],
+            states,
+            (((1,), (1,)), ((), ())),
+            preferred_element_type=f32,
+        )
+        if j + slots_head < vocab // tall:
+            head_load(j + slots_head).start()
+        if last is not None:
+            carry = gauge(j - 1, last, carry)
+        last = logits
+    top, mass, picked = gauge(vocab // tall - 1, last, carry)
+
+    def report(q, k):
+        to = {"mp": lax.rem(m + k, count), "pipe": (p if q == 0 else 1 - p)}
+        slot = q * count + k
+        return remote(stats.at[0], stats.at[slot], vs.at[slot], vr.at[slot], to)
+
+    others = [(q, k) for k in range(1, count) for q in range(2)] + [(1, 0)]
+    stats[0] = jnp.concatenate([top, mass, picked, jnp.zeros((5, length), f32)], axis=0)
+    for q, k in others:
+        report(q, k).start()
+    tallied = tallies[0]
+    for k in range(1, n):
+        tally(k).wait_recv()
+        tallied = tallied + tallies[k]
+    for q, k in others:
+        report(q, k).wait_recv()
+    peak = jnp.max(stats[:, 0, :], axis=0, keepdims=True)
+    mass = jnp.sum(stats[:, 1, :] * jnp.exp(stats[:, 0, :] - peak), axis=0, keepdims=True)
+    picked = jnp.sum(stats[:, 2, :], axis=0, keepdims=True)
+    token = picked - peak - jnp.log(mass)
+    for s in range(seq_count):
+        token_ref[s : s + 1, :] = token[:, s * seq_len : (s + 1) * seq_len]
+    lane = lax.broadcasted_iota(jnp.int32, (8, 128), 1)
+    divisor = jnp.where(lane < seq_count, tallied / (n * SEQ_MB), 1.0)
+    policy = per_sequence(mask * token) / divisor
+    anchor = per_sequence(mask * flat(anchor_ref)) / divisor
+    gaps = policy - anchor
+    policy_ref[...] = policy[:1, :seq_count]
+    losses = jnp.zeros((8, 128), f32)
+    for i in range(seq_count // 2):
+        chosen = jnp.sum(
+            jnp.where(lane == pairs_ref[0, 2 * i], gaps, 0.0), axis=1, keepdims=True
+        )
+        rejected = jnp.sum(
+            jnp.where(lane == pairs_ref[0, 2 * i + 1], gaps, 0.0), axis=1, keepdims=True
+        )
+        losses = jnp.where(lane == i, (chosen - rejected - 0.5 / ipo_tau) ** 2, losses)
+    loss_ref[...] = losses[:1, : seq_count // 2]
+    for k in range(1, n):
+        tally(k).wait_send()
+    for q, k in others:
+        report(q, k).wait_send()
+
     def drain(b, carry):
         for k in range(1, count):
             share(b, k, m).wait_send()
@@ -533,19 +570,6 @@
         return carry
 
     lax.fori_loop(0, total, drain_pieces, 0)
-
-
-def call(kernel, name, ident, outs, scratch, *args):
-    spec = pl.BlockSpec(memory_space=pltpu.VMEM)
-    return pl.pallas_call(
-        kernel,
-        name=name,
-        out_shape=outs,
-        in_specs=[spec] * len(args),
-        out_specs=jax.tree.map(lambda _: spec, outs),
-        scratch_shapes=scratch,
-        compiler_params=pltpu.CompilerParams(collective_id=ident, has_side_effects=True),
-    )(*args)
 
 
 def sems(*shape):
@@ -567,46 +591,56 @@
     seq_count, length, model_width = hidden_states.shape
     groups = lax.axis_size("dp")
     vp_size = lax.axis_size("pipe") * lax.axis_size("mp")
-    vp_index = lax.axis_index(VP)
     rows = seq_count * length
     block = model_width // groups
     ff = up_weight.shape[2]
-    mask_values = response_masks.astype(jnp.float32)
-    local_counts = jnp.sum(mask_values, axis=1)
     count = lax.axis_size("mp")
     bf16 = jnp.bfloat16
-    spread_sems = sems(count) + sems(count)
     part = rows // count
     own_rows = part * groups
     all_rows = rows * groups
     steps = BATCHES * PIECES
+    vocab = unembedding.shape[0]
     anyspec = pl.BlockSpec(memory_space=pl.ANY)
     spec = pl.BlockSpec(memory_space=pltpu.VMEM)
+    smem = pl.BlockSpec(memory_space=pltpu.SMEM)
     dma = pltpu.SemaphoreType.DMA
-    normed_final = pl.pallas_call(
+    buffers = [
+        ((rows, model_width), bf16),
+        None,
+        ((vp_size, 8, rows), jnp.float32),
+        ((groups, 8, 128), jnp.float32),
+        ((block, ff), bf16),
+        ((ff, block), bf16),
+        ((part, model_width), bf16),
+        ((part, model_width), bf16),
+        ((all_rows, block), bf16),
+        ((all_rows, ff), bf16),
+        ((all_rows, ff), bf16),
+        ((all_rows // 2, ff), bf16),
+        ((all_rows, block), bf16),
+        ((all_rows, block), bf16),
+        ((own_rows, block), bf16),
+        ((own_rows, block), bf16),
+        ((BATCHES, groups, own_rows // BATCHES, 128), jnp.float32),
+        ((BATCHES, groups, part // BATCHES, block), bf16),
+    ]
+    used = sum(math.prod(b[0]) * jnp.dtype(b[1]).itemsize for b in buffers if b)
+    tall = vocab // 8
+    kept = min(8, (ROOM - used) // (tall * model_width * 2))
+    buffers[1] = ((kept, tall, model_width), bf16)
+    token_logps, policy, losses = pl.pallas_call(
         relay_kernel,
         name="relay",
-        out_shape=jax.ShapeDtypeStruct((rows, model_width), bf16),
-        in_specs=[anyspec, anyspec, anyspec, spec, spec],
-        out_specs=spec,
-        scratch_shapes=[
-            pltpu.VMEM((block, ff), bf16),
-            pltpu.VMEM((ff, block), bf16),
-            pltpu.VMEM((part, model_width), bf16),
-            pltpu.VMEM((part, model_width), bf16),
-            pltpu.VMEM((all_rows, block), bf16),
-            pltpu.VMEM((all_rows, ff), bf16),
-            pltpu.VMEM((all_rows, ff), bf16),
-            pltpu.VMEM((all_rows // 2, ff), bf16),
-            pltpu.VMEM((all_rows, block), bf16),
-            pltpu.VMEM((all_rows, block), bf16),
-            pltpu.VMEM((own_rows, block), bf16),
-            pltpu.VMEM((own_rows, block), bf16),
-            pltpu.VMEM((BATCHES, groups, own_rows // BATCHES, 128), jnp.float32),
-            pltpu.VMEM((BATCHES, groups, part // BATCHES, block), bf16),
-            dma((3,)),
-            pltpu.SemaphoreType.REGULAR,
-        ]
+        out_shape=[
+            jax.ShapeDtypeStruct(target_ids.shape, jnp.float32),
+            jax.ShapeDtypeStruct((1, seq_count), jnp.float32),
+            jax.ShapeDtypeStruct((1, seq_count // 2), jnp.float32),
+        ],
+        in_specs=[anyspec] * 4 + [spec] * 5 + [smem],
+        out_specs=[spec] * 3,
+        scratch_shapes=[pltpu.VMEM(*b) for b in buffers]
+        + [dma((3,)), pltpu.SemaphoreType.REGULAR]
         + sems(BATCHES, groups)
         + sems(BATCHES, groups)
         + sems(BATCHES, count)
@@ -617,60 +651,26 @@
         + sems(BATCHES, groups)
         + sems(BATCHES, groups)
         + sems(BATCHES, count)
-        + sems(BATCHES, count),
+        + sems(BATCHES, count)
+        + [dma((kept,))]
+        + sems(groups)
+        + sems(vp_size),
         compiler_params=pltpu.CompilerParams(
-            collective_id=0, has_side_effects=True, vmem_limit_bytes=62 * 1024 * 1024
+            collective_id=0, has_side_effects=True, vmem_limit_bytes=67043328
         ),
     )(
         hidden_states.reshape(rows, model_width),
         up_weight[0],
         down_weight[0],
+        unembedding,
         layer_gain,
         final_gain[None],
+        target_ids,
+        response_masks,
+        anchor_logps,
+        pairing,
     )
-    logits = lax.dot_general(
-        normed_final, unembedding, (((1,), (1,)), ((), ())), preferred_element_type=jnp.float32
-    )
-    vocab_start = vp_index * unembedding.shape[0]
-    local_ids = target_ids.reshape(-1) - vocab_start
-    columns = lax.broadcasted_iota(jnp.int32, logits.shape, 1)
-    picked = jnp.sum(jnp.where(columns == local_ids[:, None], logits, 0.0), axis=1)
-    local_top = jnp.max(logits, axis=1)
-    local_sum = jnp.sum(jnp.exp(logits - local_top[:, None]), axis=1)
-    stats = jnp.pad(jnp.stack([local_top, local_sum, picked]), ((0, 5), (0, 0)))
-    padded = jnp.pad(local_counts[None], ((0, 7), (0, -seq_count % 128)))
-    stats, counts = call(
-        stats_kernel,
-        "stats",
-        1,
-        [
-            jax.ShapeDtypeStruct((vp_size * 8, rows), jnp.float32),
-            jax.ShapeDtypeStruct(padded.shape, jnp.float32),
-        ],
-        [pltpu.VMEM((groups,) + padded.shape, jnp.float32)] + sems(groups) + spread_sems,
-        stats,
-        padded,
-    )
-    stats = stats.reshape(vp_size, 8, rows)
-    counts = counts[0, :seq_count]
-    top_value = jnp.max(stats[:, 0], axis=0)
-    exp_total = jnp.sum(stats[:, 1] * jnp.exp(stats[:, 0] - top_value), axis=0)
-    picked_all = jnp.sum(stats[:, 2], axis=0)
-    token_logps = (picked_all - top_value - jnp.log(exp_total)).reshape(seq_count, length)
-
-    divisor = jnp.repeat(counts / (groups * SEQ_MB), SEQ_MB)
-    policy = jnp.sum(mask_values * token_logps, axis=1) / divisor
-    anchor = jnp.sum(mask_values * anchor_logps, axis=1) / divisor
-    log_gaps = policy - anchor
-    positions = jnp.arange(seq_count, dtype=jnp.int32)
-    chosen = jnp.sum(
-        jnp.where(pairing[0, 0::2][:, None] == positions[None, :], log_gaps[None, :], 0.0), axis=1
-    )
-    rejected = jnp.sum(
-        jnp.where(pairing[0, 1::2][:, None] == positions[None, :], log_gaps[None, :], 0.0), axis=1
-    )
-    losses = (chosen - rejected - 0.5 / ipo_tau) ** 2
-    return (token_logps, policy, losses)
+    return token_logps, policy[0], losses[0]
 
 
 def solution(mesh):

time: 195 us -> 184 us (0.944)
  matrix products: 17.5 us -> 0 us
  Pallas kernels: 167 us -> 179 us
  other arithmetic: 7.85 us -> 0 us
  local copies, waits for them, and re-layouts: 0.97 us -> 3.56 us
    dot_general x1 -> x0, matrix products: 17.5 us -> none  [shards(): lax.dot_general(normed_final, unembedding, (((1,), (1,)), ((), ())), pref...]
    pallas_call x2 -> x1, Pallas kernels: 167 us -> 179 us  [shards(): pl.pallas_call(relay_kernel, name='relay', out_shape=[jax.ShapeDtypeStruc...]
    reduce_sum x6 -> x0, other arithmetic: 4.8 us -> none  [the longest x1 3.31 us: shards(): local_sum = jnp.sum(jnp.exp(logits - local_top[:, None]), axis=1)]
    unnamed x10 -> x3, local copies, waits for them, and re-layouts: 0.02 us -> 3.56 us
where the time goes in v3:
time: 184 us
  Pallas kernels  179 us (97%)
  local copies, waits for them, and re-layouts  3.56 us (2%)
    pallas_call x1, Pallas kernels, shards(): pl.pallas_call(relay_kernel, name='relay', out_shape=[jax.ShapeDtypeStruc...  179 us

profile of v3, /device:TPU:0, one launch (start us, length us, event | category | flops | bytes accessed | tf_op | source)
XLA Modules:
  0.0 183.6 jit_solution(449446580335764946)
XLA Ops:
  0.6 179.4 %relay.1 = (f32[4,64]{1,0:T(4,128)}, f32[1,4]{1,0:T(1,128)}, f32[1,2]{1,0:T(1,128)}) custom-call(bf16[256,4096]{1,0:T(8,128)(2,1)} %bitcast.8, bf16[1024,1792]{1,0:T(8,128)(2,1)} %bitcast.6, bf16[1792,1024]{1,0:T(8,128)(2,1)} %bitcast.7, bf16[4096,4096]{1,0:T(8,128)(2,1)} %head_hbm.1, f32[1,4096]{1,0:T(1,128)} %layer_gain.1, f32[1,4096]{1,0:T(1,128)} %bitcast.9, ...), custom_call_target="tpu_custom_call" | custom-call | tf_op jit(solution)/shard_map/relay/pallas_call | solution.py:632
  180.0 1.2 copy.16
  181.3 1.1 copy.17
  182.4 1.2 copy.18

commit v4 on v3

--- a/solution.py
+++ b/solution.py
@@ -13,8 +13,9 @@
 MESH = pl.DeviceIdType.MESH
 BATCHES = 4
 PIECES = 4
-HOP = 2
-STEP = 2
+ROUND = 2 * PIECES
+HOP = 3
+STEP = 4
 ROOM = 62 * 1024 * 1024
 
 
@@ -233,20 +234,12 @@
             share(b, k, beside(k)).wait_recv()
         where = rows(b * batch, batch)
         states = xin[where, :]
-        step = 256
-        for j in range(0, ff, step):
-            hid[where, j : j + step] = jnp.dot(
-                states, up[:, j : j + step], preferred_element_type=f32
-            ).astype(hid.dtype)
+        hid[where, :] = jnp.dot(states, up[...], preferred_element_type=f32).astype(hid.dtype)
 
     def leave(b):
         where = rows(b * batch, batch)
         states = act[where, :]
-        step = min(block, 256)
-        for j in range(0, block, step):
-            outs[where, j : j + step] = jnp.dot(
-                states, down[:, j : j + step], preferred_element_type=f32
-            ).astype(outs.dtype)
+        outs[where, :] = jnp.dot(states, down[...], preferred_element_type=f32).astype(outs.dtype)
         for k in (*range(1, count), 0):
             scatter(b, k).start()
 
@@ -303,7 +296,7 @@
 
     offset = 2 * STEP + 1
     deep = HOP * (n // 2)
-    ticks = offset + total + 2 * deep
+    ticks = offset + 2 * total + 2 * deep
 
     def tick(t, carry):
         now = t - offset
@@ -311,9 +304,10 @@
             owner = n // 2 - way
             left, right = d < owner, d > owner
             hops = jnp.where(left, d, n - 1 - d)
-            c = now - HOP * hops
-
-            @pl.when((d != owner) & (c >= 0) & (c < total))
+            late = now - way - HOP * hops
+            c = lax.div(late, 2)
+
+            @pl.when((d != owner) & (late >= 0) & (lax.rem(late, 2) == 0) & (c < total))
             def _():
                 here = span(way, c)
 
@@ -340,9 +334,10 @@
 
         for way in range(2):
             owner = n // 2 - way
-            c = now - deep
-
-            @pl.when((d == owner) & (c >= 0) & (c < total))
+            late = now - way - deep
+            c = lax.div(late, 2)
+
+            @pl.when((d == owner) & (late >= 0) & (lax.rem(late, 2) == 0) & (c < total))
             def _():
                 here = span(way, c)
                 there = rows(c * piece, piece)
@@ -367,9 +362,10 @@
             owner = n // 2 - way
             left, right = d < owner, d > owner
             away = jnp.where(left, owner - d, d - owner)
-            c = now - deep - HOP * away
-
-            @pl.when((d != owner) & (c >= 0) & (c < total))
+            late = now - way - deep - HOP * away
+            c = lax.div(late, 2)
+
+            @pl.when((d != owner) & (late >= 0) & (lax.rem(late, 2) == 0) & (c < total))
             def _():
                 outer(way, c, 0).wait_recv()
 
@@ -381,30 +377,30 @@
                 def _():
                     outer(way, c, 1).start()
 
-        b = lax.div(now + 1, PIECES)
-
-        @pl.when((now + 1 >= 0) & (lax.rem(now + 1, PIECES) == 0) & (b < BATCHES))
+        b = lax.div(now + 1, ROUND)
+
+        @pl.when((now + 1 >= 0) & (lax.rem(now + 1, ROUND) == 0) & (b < BATCHES))
         def _():
             enter(b)
 
-        done = now - (PIECES - 1) - 2 * deep
-        q = lax.div(done, PIECES)
-
-        @pl.when((done >= 0) & (lax.rem(done, PIECES) == 0) & (q < BATCHES))
+        done = now - (ROUND - 1) - 2 * deep
+        q = lax.div(done, ROUND)
+
+        @pl.when((done >= 0) & (lax.rem(done, ROUND) == 0) & (q < BATCHES))
         def _():
             leave(q)
 
         late = now + 1 + STEP
-        e = lax.div(late, PIECES)
-
-        @pl.when((p == 1) & (late >= 0) & (lax.rem(late, PIECES) == 0) & (e < BATCHES))
+        e = lax.div(late, ROUND)
+
+        @pl.when((p == 1) & (late >= 0) & (lax.rem(late, ROUND) == 0) & (e < BATCHES))
         def _():
             renew(e)
 
         early = now + 1 + 2 * STEP
-        a = lax.div(early, PIECES)
-
-        @pl.when((p == 1) & (lax.rem(early, PIECES) == 0) & (a < BATCHES))
+        a = lax.div(early, ROUND)
+
+        @pl.when((p == 1) & (lax.rem(early, ROUND) == 0) & (a < BATCHES))
         def _():
             settle(a)
 
@@ -469,11 +465,17 @@
     last = None
     for j in range(vocab // tall):
         head_load(j).wait()
-        logits = lax.dot_general(
-            head[j % slots_head],
-            states,
-            (((1,), (1,)), ((), ())),
-            preferred_element_type=f32,
+        logits = jnp.concatenate(
+            [
+                lax.dot_general(
+                    head[j % slots_head, cut : cut + tall // 2],
+                    states,
+                    (((1,), (1,)), ((), ())),
+                    preferred_element_type=f32,
+                )
+                for cut in (0, tall // 2)
+            ],
+            axis=0,
         )
         if j + slots_head < vocab // tall:
             head_load(j + slots_head).start()

time: 184 us -> 169 us (0.918)
  Pallas kernels: 179 us -> 165 us
    pallas_call x1, Pallas kernels: 179 us -> 165 us  [shards(): pl.pallas_call(relay_kernel, name='relay', out_shape=[jax.ShapeDtypeStruc...]
where the time goes in v4:
time: 169 us
  Pallas kernels  165 us (98%)
  local copies, waits for them, and re-layouts  3.56 us (2%)
    pallas_call x1, Pallas kernels, shards(): pl.pallas_call(relay_kernel, name='relay', out_shape=[jax.ShapeDtypeStruc...  165 us
    unnamed x3, local copies, waits for them, and re-layouts  3.56 us

profile of v4, /device:TPU:0, one launch (start us, length us, event | category | flops | bytes accessed | tf_op | source)
XLA Modules:
  0.0 169.0 jit_solution(4574102982172779997)
XLA Ops:
  0.6 164.8 %relay.1 = (f32[4,64]{1,0:T(4,128)}, f32[1,4]{1,0:T(1,128)}, f32[1,2]{1,0:T(1,128)}) custom-call(bf16[256,4096]{1,0:T(8,128)(2,1)} %bitcast.8, bf16[1024,1792]{1,0:T(8,128)(2,1)} %bitcast.6, bf16[1792,1024]{1,0:T(8,128)(2,1)} %bitcast.7, bf16[4096,4096]{1,0:T(8,128)(2,1)} %head_hbm.1, f32[1,4096]{1,0:T(1,128)} %layer_gain.1, f32[1,4096]{1,0:T(1,128)} %bitcast.9, ...), custom_call_target="tpu_custom_call" | custom-call | tf_op jit(solution)/shard_map/relay/pallas_call | solution.py:634
  165.4 1.2 copy.16
  166.7 1.1 copy.17
  167.8 1.2 copy.18

commit v5 on v4

--- a/solution.py
+++ b/solution.py
@@ -1,3 +1,4 @@
+import functools
 import math
 import jax
 import jax.numpy as jnp
@@ -16,7 +17,7 @@
 ROUND = 2 * PIECES
 HOP = 3
 STEP = 4
-ROOM = 62 * 1024 * 1024
+ROOM = 59 * 1024 * 1024
 
 
 def remote(src, dst, send_sem, recv_sem, target):
@@ -52,10 +53,53 @@
     pl.semaphore_wait(barrier, n - 1 + count - 1 + count)
 
 
+def flat(ref):
+    return jnp.concatenate([ref[s : s + 1, :] for s in range(ref.shape[0])], axis=1)
+
+
+def per_sequence(row, seq_len):
+    length = row.shape[1]
+    lanes = lax.broadcasted_iota(jnp.int32, (length, 128), 1)
+    spots = lax.broadcasted_iota(jnp.int32, (length, 128), 0)
+    return lax.dot_general(
+        jnp.broadcast_to(row, (8, length)),
+        (lanes == spots // seq_len).astype(jnp.float32),
+        (((1,), (0,)), ((), ())),
+        precision=lax.Precision.HIGHEST,
+        preferred_element_type=jnp.float32,
+    )
+
+
+def close_kernel(n, result_ref, mask_ref, anchor_ref, pairs_ref, token_ref, policy_ref, loss_ref):
+    f32 = jnp.float32
+    seq_count, seq_len = mask_ref.shape
+    mask = flat(mask_ref).astype(f32)
+    token = result_ref[:1, :]
+    tallied = result_ref[1:2, :128]
+    for s in range(seq_count):
+        token_ref[s : s + 1, :] = token[:, s * seq_len : (s + 1) * seq_len]
+    lane = lax.broadcasted_iota(jnp.int32, (8, 128), 1)
+    divisor = jnp.where(lane < seq_count, tallied / (n * SEQ_MB), 1.0)
+    policy = per_sequence(mask * token, seq_len) / divisor
+    anchor = per_sequence(mask * flat(anchor_ref), seq_len) / divisor
+    gaps = policy - anchor
+    policy_ref[...] = policy[:1, :seq_count]
+    losses = jnp.zeros((8, 128), f32)
+    for i in range(seq_count // 2):
+        chosen = jnp.sum(
+            jnp.where(lane == pairs_ref[0, 2 * i], gaps, 0.0), axis=1, keepdims=True
+        )
+        rejected = jnp.sum(
+            jnp.where(lane == pairs_ref[0, 2 * i + 1], gaps, 0.0), axis=1, keepdims=True
+        )
+        losses = jnp.where(lane == i, (chosen - rejected - 0.5 / ipo_tau) ** 2, losses)
+    loss_ref[...] = losses[:1, : seq_count // 2]
+
+
 def relay_kernel(
-    x_hbm, up_hbm, down_hbm, head_hbm, layer_gain, final_gain, ids_ref, mask_ref, anchor_ref,
-    pairs_ref, token_ref, policy_ref, loss_ref, full_ref, head, stats, tallies, up, down, xs, normed, xin, hid, act, ext, outs, rs, resid, nxt, slots, fin,
-    load, go, ns, nr, xs_s, xs_r, gs, gr, ins, inr, exr, bs, br, rss, rsr, ds, dr, qs, qr,
+    x_hbm, up_hbm, down_hbm, head_hbm, layer_gain, final_gain, ids_ref, mask_ref,
+    out_ref, full_ref, head, stats, tallies, up, down, xs, normed, xin, hid, act, ext, outs, rs, resid, nxt, slots, fin, scales,
+    load, go, cs, cr, ns, nr, xs_s, xs_r, gs, gr, ins, inr, exr, bs, br, rss, rsr, ds, dr, qs, qr,
     hs, hr, fs, fr, es, er, load_head, ts, tr, vs, vr,
 ):
     n, count = lax.axis_size("dp"), lax.axis_size("mp")
@@ -87,23 +131,8 @@
     meet()
     seq_count, seq_len = mask_ref.shape
 
-    def flat(ref):
-        return jnp.concatenate([ref[s : s + 1, :] for s in range(seq_count)], axis=1)
-
-    lanes = lax.broadcasted_iota(jnp.int32, (length, 128), 1)
-    member = (lanes == lax.broadcasted_iota(jnp.int32, (length, 128), 0) // seq_len).astype(f32)
-
-    def per_sequence(row):
-        return lax.dot_general(
-            jnp.broadcast_to(row, (8, length)),
-            member,
-            (((1,), (0,)), ((), ())),
-            precision=lax.Precision.HIGHEST,
-            preferred_element_type=f32,
-        )
-
     mask = flat(mask_ref).astype(f32)
-    tallies[0] = per_sequence(mask)
+    tallies[0] = per_sequence(mask, seq_len)
 
     def tally(k):
         return remote(
@@ -135,6 +164,19 @@
     def share(b, k, owner):
         slab = xin.at[rows(b * batch + owner * own_rows, own_rows)]
         return remote(slab, slab, gs.at[b, k], gr.at[b, k], {"mp": lax.rem(m + k, count)})
+
+    def pass_on(b, k, owner):
+        return remote(
+            nxt.at[rows(b * own_rows, own_rows)],
+            xin.at[rows(b * batch + owner * own_rows, own_rows)],
+            gs.at[b, k],
+            gr.at[b, k],
+            {"mp": lax.rem(m + k, count)},
+        )
+
+    def pass_scale(b, k, owner):
+        slab = scales.at[rows(b * batch + owner * own_rows, own_rows)]
+        return remote(slab, slab, cs.at[b, k], cr.at[b, k], {"mp": lax.rem(m + k, count)})
 
     def scatter(b, k):
         to = lax.rem(m + k, count)
@@ -230,9 +272,22 @@
         head_load(j).start()
 
     def enter(b):
-        for k in range(1, count):
-            share(b, k, beside(k)).wait_recv()
         where = rows(b * batch, batch)
+
+        @pl.when(p == 0)
+        def _():
+            for k in range(1, count):
+                share(b, k, beside(k)).wait_recv()
+
+        @pl.when(p == 1)
+        def _():
+            for k in range(1, count):
+                pass_on(b, k, beside(k)).wait_recv()
+                pass_scale(b, k, beside(k)).wait_recv()
+            xin[where, :] = (
+                xin[where, :].astype(f32) * scales[where, :1] * layer_gain[:, columns(d)]
+            ).astype(xin.dtype)
+
         states = xin[where, :]
         hid[where, :] = jnp.dot(states, up[...], preferred_element_type=f32).astype(hid.dtype)
 
@@ -262,19 +317,19 @@
         slots[b, 0] = jnp.broadcast_to(sums, (own_rows, 128))
         for k in range(1, n):
             square(b, k).start()
+        for k in range(1, count):
+            pass_on(b, k, m).start()
         hand_over(b).start()
+        xin[rows(b * batch + m * own_rows, own_rows), :] = wide.astype(xin.dtype)
 
     def renew(b):
         sums = slots[b, 0]
         for k in range(1, n):
             square(b, k).wait_recv()
             sums = sums + slots[b, k]
-        scale = lax.rsqrt(sums[:, :1] / width + epsilon)
-        wide = nxt[rows(b * own_rows, own_rows), :].astype(f32)
-        gain = layer_gain[:, columns(d)]
-        xin[rows(b * batch + m * own_rows, own_rows), :] = (wide * scale * gain).astype(xin.dtype)
+        scales[rows(b * batch + m * own_rows, own_rows), :] = lax.rsqrt(sums / width + epsilon)
         for k in range(1, count):
-            share(b, k, m).start()
+            pass_scale(b, k, m).start()
 
     def span(way, c):
         b, k = lax.div(c, PIECES), lax.rem(c, PIECES)
@@ -503,37 +558,21 @@
     mass = jnp.sum(stats[:, 1, :] * jnp.exp(stats[:, 0, :] - peak), axis=0, keepdims=True)
     picked = jnp.sum(stats[:, 2, :], axis=0, keepdims=True)
     token = picked - peak - jnp.log(mass)
-    for s in range(seq_count):
-        token_ref[s : s + 1, :] = token[:, s * seq_len : (s + 1) * seq_len]
-    lane = lax.broadcasted_iota(jnp.int32, (8, 128), 1)
-    divisor = jnp.where(lane < seq_count, tallied / (n * SEQ_MB), 1.0)
-    policy = per_sequence(mask * token) / divisor
-    anchor = per_sequence(mask * flat(anchor_ref)) / divisor
-    gaps = policy - anchor
-    policy_ref[...] = policy[:1, :seq_count]
-    losses = jnp.zeros((8, 128), f32)
-    for i in range(seq_count // 2):
-        chosen = jnp.sum(
-            jnp.where(lane == pairs_ref[0, 2 * i], gaps, 0.0), axis=1, keepdims=True
-        )
-        rejected = jnp.sum(
-            jnp.where(lane == pairs_ref[0, 2 * i + 1], gaps, 0.0), axis=1, keepdims=True
-        )
-        losses = jnp.where(lane == i, (chosen - rejected - 0.5 / ipo_tau) ** 2, losses)
-    loss_ref[...] = losses[:1, : seq_count // 2]
+    out_ref[:1, :] = token
+    out_ref[1:2, :128] = tallied[:1]
     for k in range(1, n):
         tally(k).wait_send()
     for q, k in others:
         report(q, k).wait_send()
 
     def drain(b, carry):
-        for k in range(1, count):
-            share(b, k, m).wait_send()
         for k in range(count):
             scatter(b, k).wait_send()
 
         @pl.when(p == 0)
         def _():
+            for k in range(1, count):
+                share(b, k, m).wait_send()
             for k in range(1, n):
                 first_hop(b, k, d).wait_send()
                 last_hop(b, k, d).wait_send()
@@ -547,6 +586,9 @@
             for k in range(1, n):
                 plain_hop(b, k, d).wait_send()
                 square(b, k).wait_send()
+            for k in range(1, count):
+                pass_on(b, k, m).wait_send()
+                pass_scale(b, k, m).wait_send()
             hand_over(b).wait_send()
 
         return carry
@@ -626,23 +668,24 @@
         ((own_rows, block), bf16),
         ((BATCHES, groups, own_rows // BATCHES, 128), jnp.float32),
         ((BATCHES, groups, part // BATCHES, block), bf16),
+        ((all_rows, 128), jnp.float32),
     ]
     used = sum(math.prod(b[0]) * jnp.dtype(b[1]).itemsize for b in buffers if b)
-    tall = vocab // 8
-    kept = min(8, (ROOM - used) // (tall * model_width * 2))
+    cuts = 8
+    while used + vocab // cuts * model_width * 2 > ROOM:
+        cuts *= 2
+    tall = vocab // cuts
+    kept = min(cuts, (ROOM - used) // (tall * model_width * 2))
     buffers[1] = ((kept, tall, model_width), bf16)
-    token_logps, policy, losses = pl.pallas_call(
+    result = pl.pallas_call(
         relay_kernel,
         name="relay",
-        out_shape=[
-            jax.ShapeDtypeStruct(target_ids.shape, jnp.float32),
-            jax.ShapeDtypeStruct((1, seq_count), jnp.float32),
-            jax.ShapeDtypeStruct((1, seq_count // 2), jnp.float32),
-        ],
-        in_specs=[anyspec] * 4 + [spec] * 5 + [smem],
-        out_specs=[spec] * 3,
+        out_shape=jax.ShapeDtypeStruct((2, rows), jnp.float32),
+        in_specs=[anyspec] * 4 + [spec] * 4,
+        out_specs=spec,
         scratch_shapes=[pltpu.VMEM(*b) for b in buffers]
         + [dma((3,)), pltpu.SemaphoreType.REGULAR]
+        + sems(BATCHES, count)
         + sems(BATCHES, groups)
         + sems(BATCHES, groups)
         + sems(BATCHES, count)
@@ -669,9 +712,18 @@
         final_gain[None],
         target_ids,
         response_masks,
-        anchor_logps,
-        pairing,
     )
+    token_logps, policy, losses = pl.pallas_call(
+        functools.partial(close_kernel, groups),
+        name="close",
+        out_shape=[
+            jax.ShapeDtypeStruct(target_ids.shape, jnp.float32),
+            jax.ShapeDtypeStruct((1, seq_count), jnp.float32),
+            jax.ShapeDtypeStruct((1, seq_count // 2), jnp.float32),
+        ],
+        in_specs=[spec] * 3 + [smem],
+        out_specs=[spec] * 3,
+    )(result, response_masks, anchor_logps, pairing)
     return token_logps, policy[0], losses[0]
 
 

time: 169 us -> 166 us (0.982)
  local copies, waits for them, and re-layouts: 3.56 us -> 0 us
    unnamed x3 -> x0, local copies, waits for them, and re-layouts: 3.56 us -> none
    pallas_call x1 -> x2, Pallas kernels: 165 us -> 165 us  [the longest x1 164 us: shards(): pl.pallas_call(relay_kernel, name='relay', out_shape=jax.ShapeDtypeStruct...]
where the time goes in v5:
time: 166 us
  Pallas kernels  165 us (99%)
    pallas_call x1, Pallas kernels, shards(): pl.pallas_call(relay_kernel, name='relay', out_shape=jax.ShapeDtypeStruct...  164 us

profile of v5, /device:TPU:0, one launch (start us, length us, event | category | flops | bytes accessed | tf_op | source)
XLA Modules:
  0.0 166.1 jit_solution(16749957745529931329)
XLA Ops:
  0.6 163.7 %relay.1.result_ref = f32[2,256]{1,0:T(2,128)} custom-call(bf16[256,4096]{1,0:T(8,128)(2,1)} %bitcast.8, bf16[1024,1792]{1,0:T(8,128)(2,1)} %bitcast.6, bf16[1792,1024]{1,0:T(8,128)(2,1)} %bitcast.7, bf16[4096,4096]{1,0:T(8,128)(2,1)} %head_hbm.1, f32[1,4096]{1,0:T(1,128)} %layer_gain.1, f32[1,4096]{1,0:T(1,128)} %bitcast.9, s32[4,64]{1,0:T(4,128)} %ids_ref.1, ...), custom_call_target="tpu_custom_call" | custom-call | tf_op jit(solution)/shard_map/relay/pallas_call | solution.py:680
  164.3 1.7 %close.1 = (f32[4,64]{1,0:T(4,128)}, f32[1,4]{1,0:T(1,128)}, f32[1,2]{1,0:T(1,128)}) custom-call(f32[2,256]{1,0:T(2,128)} %relay.1.result_ref, s32[4,64]{1,0:T(4,128)} %mask_ref.3, f32[4,64]{1,0:T(4,128)} %anchor_ref.1, s32[1,4]{1,0:T(1,128)} %pairs_ref.1), custom_call_target="tpu_custom_call" | custom-call | tf_op jit(solution)/shard_map/close/pallas_call | solution.py:716

commit v6 on v5

--- a/solution.py
+++ b/solution.py
@@ -229,10 +229,11 @@
 
     @pl.when(p == 0)
     def _():
-        wide = xs[...].astype(f32)
-        scale = lax.rsqrt(jnp.mean(wide * wide, axis=-1, keepdims=True) + epsilon)
-        normed[...] = (wide * scale * layer_gain[...]).astype(normed.dtype)
         for b in range(BATCHES):
+            cut = slice(b * sub, (b + 1) * sub)
+            wide = xs[cut, :].astype(f32)
+            scale = lax.rsqrt(jnp.mean(wide * wide, axis=-1, keepdims=True) + epsilon)
+            normed[cut, :] = (wide * scale * layer_gain[...]).astype(normed.dtype)
             for k in range(1, n):
                 first_hop(b, k, d).start()
         for b in range(BATCHES):

time: 166 us -> 166 us (level)
  no operation moved by 1% of the time
where the time goes in v6:
time: 166 us
  Pallas kernels  165 us (99%)
    pallas_call x1, Pallas kernels, shards(): pl.pallas_call(relay_kernel, name='relay', out_shape=jax.ShapeDtypeStruct...  164 us

profile of v6, /device:TPU:0, one launch (start us, length us, event | category | flops | bytes accessed | tf_op | source)
XLA Modules:
  0.0 166.0 jit_solution(4098870692429635605)
XLA Ops:
  0.6 163.6 %relay.1.result_ref = f32[2,256]{1,0:T(2,128)} custom-call(bf16[256,4096]{1,0:T(8,128)(2,1)} %bitcast.8, bf16[1024,1792]{1,0:T(8,128)(2,1)} %bitcast.6, bf16[1792,1024]{1,0:T(8,128)(2,1)} %bitcast.7, bf16[4096,4096]{1,0:T(8,128)(2,1)} %head_hbm.1, f32[1,4096]{1,0:T(1,128)} %layer_gain.1, f32[1,4096]{1,0:T(1,128)} %bitcast.9, s32[4,64]{1,0:T(4,128)} %ids_ref.1, ...), custom_call_target="tpu_custom_call" | custom-call | tf_op jit(solution)/shard_map/relay/pallas_call | solution.py:681
  164.2 1.7 %close.1 = (f32[4,64]{1,0:T(4,128)}, f32[1,4]{1,0:T(1,128)}, f32[1,2]{1,0:T(1,128)}) custom-call(f32[2,256]{1,0:T(2,128)} %relay.1.result_ref, s32[4,64]{1,0:T(4,128)} %mask_ref.3, f32[4,64]{1,0:T(4,128)} %anchor_ref.1, s32[1,4]{1,0:T(1,128)} %pairs_ref.1), custom_call_target="tpu_custom_call" | custom-call | tf_op jit(solution)/shard_map/close/pallas_call | solution.py:717
